TPU v7x, 256 devices: a whole 4x4x8 slice. The times are simulated.
256 devices in a mesh: rp: 8 (over x, z_lo), pb: 32 (over z_hi, y, core).
Axes of the slice: x: 4, y: 4, z: 8 (z_hi: 4, z_lo: 2; z = z_hi * 2 + z_lo), core: 2. Of those that a mesh axis runs over, the one named last changes fastest.
Arguments:
- wannier_g: bfloat16 [2, 1024, 32, 1152], P(None, 'rp', 'pb'), may hold values from -0.19921875 to 0.19921875
- rp_coords: int32 [3, 1024], replicated, may hold values from -8 to 8
- q_coords: int32 [3, 512], P(None, ('rp', 'pb')), may hold values from 0 to 15
- k_index: int32 [1], replicated, may hold values from 0 to 7
- k_vectors: bfloat16 [8, 2, 32, 32], replicated, may hold values from -0.75 to 0.75
- kq_vectors: bfloat16 [512, 2, 32, 32], P(('rp', 'pb')), may hold values from -0.75 to 0.75
- modes: bfloat16 [512, 2, 36, 36], P(('rp', 'pb')), may hold values from -0.75 to 0.75
Outputs:
- rotated: float32 [512, 2, 32, 1152], P(('rp', 'pb'))
All inputs are finite; a program needn't handle non-finite values.
Results may differ from a plain program's by a relative error of at most 0.0054.
Values may be sent and summed in bfloat16 or wider, within the bound.
No kernel may reach another device: no remote copies, remote signals or barrier semaphores. Data moves between devices by JAX's collectives and lax.ppermute only.
A program may use at most 64 MiB of HBM per device.

v0:
```python
import math

import jax
import jax.numpy as jnp
from jax import lax
from jax.sharding import PartitionSpec as P

NK = 16


def in_blocks(x, dim, length):
    shape = x.shape
    parts = x.reshape(*shape[:dim], length, shape[dim] // length, *shape[dim + 1 :])
    return jnp.moveaxis(parts, dim, 0)


def joined_along(parts, dim):
    shape = list(parts.shape[1:])
    shape[dim] *= parts.shape[0]
    return jnp.moveaxis(parts, 0, dim).reshape(shape)


def one_exchange(x, axis, axes, splits, concats):
    sizes = [lax.axis_size(a) for a in axes]
    parts = in_blocks(x, splits[0], sizes[0])
    parts = jnp.moveaxis(in_blocks(parts, splits[1] + 1, sizes[1]), 0, 1)
    inside = parts.shape[2:]
    parts = parts.reshape(-1, *inside)
    parts = lax.all_to_all(parts, axis, split_axis=0, concat_axis=0, tiled=True)
    parts = joined_along(parts.reshape(*sizes, *inside), concats[0] + 1)
    return joined_along(parts, concats[1])


def phases(q_rows, r_coords):
    turns = jnp.mod(jnp.sum(q_rows[:, :, None] * r_coords[:, None, :], axis=0), NK)
    angle = turns.astype(jnp.float32) * (2.0 * math.pi / NK)
    cosine = jnp.cos(angle).astype(jnp.bfloat16)
    sine = jnp.sin(angle).astype(jnp.bfloat16)
    return (jnp.concatenate([cosine, -sine], axis=1), jnp.concatenate([sine, cosine], axis=1))


def rotate(fourier, mode_vecs, unit, kq_vecs):
    count = fourier.shape[0]
    bands = kq_vecs.shape[2]
    branches = mode_vecs.shape[2]
    field = fourier.reshape(count, 2, bands, bands, branches)
    e_real, e_imag = (mode_vecs[:, 0], mode_vecs[:, 1])
    e_block = jnp.stack([jnp.stack([e_real, e_imag], 2), jnp.stack([-e_imag, e_real], 2)], 1)
    by_mode = jnp.einsum(
        "qcmnv,qcvdu->qdmnu", field, e_block, preferred_element_type=jnp.float32
    ).astype(jnp.bfloat16)
    u_real, u_imag = (unit[0], unit[1])
    u_block = jnp.stack([jnp.stack([u_real, u_imag], 1), jnp.stack([-u_imag, u_real], 1)], 0)
    by_band = jnp.einsum(
        "qcmnu,cndj->qdmju", by_mode, u_block, preferred_element_type=jnp.float32
    ).astype(jnp.bfloat16)
    v_real, v_imag = (kq_vecs[:, 0], kq_vecs[:, 1])
    v_block = jnp.stack([jnp.stack([v_real, -v_imag], 2), jnp.stack([v_imag, v_real], 2)], 1)
    result = jnp.einsum("qcmju,qcmdi->qdiju", by_band, v_block, preferred_element_type=jnp.float32)
    return result.reshape(count, 2, bands, bands * branches)


def local(wannier_g, rp_coords, q_coords, k_index, k_vectors, kq_vectors, modes):
    q_all = lax.all_gather(q_coords, ("rp", "pb"), axis=1, tiled=True)
    total = q_all.shape[1]
    groups = lax.axis_size("rp")
    block = total // groups
    moved = lax.all_to_all(wannier_g, "rp", split_axis=3, concat_axis=1, tiled=True)
    right = moved.reshape(2 * moved.shape[1], -1)
    q_blocks = q_all.reshape(3, groups, block).transpose(1, 0, 2)

    def fourier_block(q_rows):
        left_real, left_imag = phases(q_rows, rp_coords)
        f_real = jnp.dot(left_real, right, preferred_element_type=jnp.float32).astype(jnp.bfloat16)
        f_imag = jnp.dot(left_imag, right, preferred_element_type=jnp.float32).astype(jnp.bfloat16)
        return jnp.stack([f_real, f_imag], 1)

    fourier = lax.map(fourier_block, q_blocks).reshape(total, 2, moved.shape[2], moved.shape[3])
    owned = one_exchange(fourier, ("rp", "pb"), ("rp", "pb"), (0, 0), (3, 2))
    select = (jnp.arange(k_vectors.shape[0]) == k_index[0]).astype(jnp.bfloat16)
    unit = jnp.einsum("k,kcnj->cnj", select, k_vectors, preferred_element_type=jnp.float32).astype(
        jnp.bfloat16
    )
    return rotate(owned, modes, unit, kq_vectors)


def solution(mesh):
    return jax.shard_map(
        local,
        mesh=mesh,
        in_specs=(
            P(None, "rp", "pb", None),
            P(),
            P(None, ("rp", "pb")),
            P(),
            P(),
            P(("rp", "pb"), None, None, None),
            P(("rp", "pb"), None, None, None),
        ),
        out_specs=P(("rp", "pb"), None, None, None),
        check_vma=False,
    )
```

profile of v0, /device:TPU:1, one launch (start us, length us, event | category | flops | bytes accessed | tf_op | source)
XLA Modules:
  0.0 424.2 jit_solution(9630580377085636037)
XLA Ops:
  0.0 3.0 copy.101
  3.0 6.2 %all-to-all-start = ((bf16[2,128,1,1152]{1,0,2,3:T(2,128)(2,1)}), bf16[2,128,1,1152]{1,0,2,3:T(2,128)(2,1)S(1)}, u32[]{:S(2)}, u32[]{:S(2)}) async-start(bf16[2,128,1,1152]{1,0,2,3:T(2,128)(2,1)} %copy.101), calls=%async_computation | async-start | bytes 1179648 | tf_op jit(solution)/shard_map/all_to_all | solution.py:68
  10.3 350.8 %all-gather = s32[256,2,3]{2,1,0:T(2,128)S(1)} all-gather(s32[1,2,3]{2,1,0:T(2,128)S(1)} %bitcast.145), channel_id=1, replica_groups=mesh['rp'=8,'pb'=32] {'rp','pb'}, dimensions={0}, use_global_device_ids=true | all-gather | bytes 6168 | tf_op jit(solution)/shard_map/all_gather | solution.py:64
  362.0 27.2 %while.12 = (s32[]{:T(128)}, bf16[8,64,2,144]{3,2,1,0:T(2,128)(2,1)}, s32[8,3,64]{2,0,1:T(8,128)S(1)}, s32[3,1024]{1,0:T(4,128)S(1)}, bf16[2048,144]{1,0:T(8,128)(2,1)S(1)}, /*index=5*/s32[]{:T(128)}) while((s32[]{:T(128)}, bf16[8,64,2,144]{3,2,1,0:T(2,128)(2,1)}, s32[8,3,64]{2,0,1:T(8,128)S(1)}, s32[3,1024]{1,0:T(4,128)S(1)}, ...), condition=%wide.region_2.3_spmd, body=%wide.region_0.2_spmd.sunk | while | flops 78942208 | bytes 3112789 | solution.py:78
  362.1 0.9 cosine_convert_fusion.2
  363.1 1.0 fusion.51
  364.7 0.7 copy_dynamic-update-slice_fusion.2
  365.5 0.9 cosine_convert_fusion.2
  366.5 1.0 fusion.51
  368.1 0.7 copy_dynamic-update-slice_fusion.2
  368.9 0.9 cosine_convert_fusion.2
  369.9 1.0 fusion.51
  371.5 0.7 copy_dynamic-update-slice_fusion.2
  372.3 0.9 cosine_convert_fusion.2
  373.3 1.0 fusion.51
  375.7 0.9 cosine_convert_fusion.2
  376.6 1.0 fusion.51
  378.2 0.7 copy_dynamic-update-slice_fusion.2
  379.1 0.9 cosine_convert_fusion.2
  380.0 1.0 fusion.51
  381.6 0.7 copy_dynamic-update-slice_fusion.2
  382.5 0.9 cosine_convert_fusion.2
  383.4 1.0 fusion.51
  385.0 0.7 copy_dynamic-update-slice_fusion.2
  385.9 0.9 cosine_convert_fusion.2
  386.8 1.0 fusion.51
  388.4 0.7 copy_dynamic-update-slice_fusion.2
  389.1 5.3 %all-to-all-start.1 = ((bf16[256,2,2,1,144]{4,2,1,3,0:T(2,128)(2,1)}), bf16[256,2,2,1,144]{4,2,1,3,0:T(2,128)(2,1)S(1)}, u32[]{:S(2)}, u32[]{:S(2)}) async-start(bf16[256,2,2,1,144]{4,2,1,3,0:T(2,128)(2,1)} %bitcast.38), calls=%async_computation.1 | async-start | bytes 1048576 | tf_op jit(solution)/shard_map/all_to_all | solution.py:29
  394.9 20.4 %all-to-all-done.1 = bf16[256,2,2,1,144]{4,2,1,3,0:T(2,128)(2,1)S(1)} async-done(((bf16[256,2,2,1,144]{4,2,1,3,0:T(2,128)(2,1)}), bf16[256,2,2,1,144]{4,2,1,3,0:T(2,128)(2,1)S(1)}, u32[]{:S(2)}, u32[]{:S(2)}) %all-to-all-start.1) | async-done | bytes 294944 | tf_op jit(solution)/shard_map/all_to_all | solution.py:29
  416.2 2.8 reshape_reshape.3
  420.5 1.2 copy.114
  421.7 2.4 reshape.53
  (86 shorter events, 10.5 us)
Async XLA Ops:
  0.0 9.9 %copy-start = (bf16[8,2,32,32]{3,2,1,0:T(8,128)(2,1)S(1)}, bf16[8,2,32,32]{3,2,1,0:T(8,128)(2,1)}, u32[]{:S(2)}) copy-start(bf16[8,2,32,32]{3,2,1,0:T(8,128)(2,1)} %param.13) | copy-start | bytes 98308
  0.0 10.2 %copy-start.3 = (bf16[2,2,32,32]{3,2,1,0:T(8,128)(2,1)S(1)}, bf16[2,2,32,32]{3,2,1,0:T(8,128)(2,1)}, u32[]{:S(2)}) copy-start(bf16[2,2,32,32]{3,2,1,0:T(8,128)(2,1)} %param.14) | copy-start | bytes 24580
  0.0 10.3 %copy-start.4 = (s32[3,2]{0,1:T(2,128)S(1)}, s32[3,2]{0,1:T(2,128)}, u32[]{:S(2)}) copy-start(s32[3,2]{0,1:T(2,128)} %param.11) | copy-start | bytes 76
  0.0 361.3 %copy-start.2 = (bf16[2,2,36,36]{3,1,2,0:T(2,128)(2,1)S(1)}, bf16[2,2,36,36]{3,1,2,0:T(2,128)(2,1)}, u32[]{:S(2)}) copy-start(bf16[2,2,36,36]{3,1,2,0:T(2,128)(2,1)} %param.15) | copy-start | bytes 31108
  3.0 358.3 %all-to-all-start = ((bf16[2,128,1,1152]{1,0,2,3:T(2,128)(2,1)}), bf16[2,128,1,1152]{1,0,2,3:T(2,128)(2,1)S(1)}, u32[]{:S(2)}, u32[]{:S(2)}) async-start(bf16[2,128,1,1152]{1,0,2,3:T(2,128)(2,1)} %copy.101), calls=%async_computation | async-start | bytes 1179648 | tf_op jit(solution)/shard_map/all_to_all | solution.py:68
  9.2 352.8 %copy-start.1 = (s32[3,1024]{1,0:T(4,128)S(1)}, s32[3,1024]{1,0:T(4,128)}, u32[]{:S(2)}) copy-start(s32[3,1024]{1,0:T(4,128)} %param.10) | copy-start | bytes 36868
  389.1 26.2 %all-to-all-start.1 = ((bf16[256,2,2,1,144]{4,2,1,3,0:T(2,128)(2,1)}), bf16[256,2,2,1,144]{4,2,1,3,0:T(2,128)(2,1)S(1)}, u32[]{:S(2)}, u32[]{:S(2)}) async-start(bf16[256,2,2,1,144]{4,2,1,3,0:T(2,128)(2,1)} %bitcast.38), calls=%async_computation.1 | async-start | bytes 1048576 | tf_op jit(solution)/shard_map/all_to_all | solution.py:29
where the time goes:
time: 424 us
  blocking collectives  351 us (83%)
  waiting for transfers between devices  20.4 us (5%)
  local copies, waits for them, and re-layouts  17 us (4%)
  other arithmetic  16.8 us (4%)
  starting transfers between devices  11.5 us (3%)
  matrix products  6.36 us (2%)
    all_gather x1, blocking collectives, local(): q_all = lax.all_gather(q_coords, ('rp', 'pb'), axis=1, tiled=True)  351 us
    all_to_all x1, waiting for transfers between devices, one_exchange(): parts = lax.all_to_all(parts, axis, split_axis=0, concat_axis=0, tiled=True)  20.4 us
  transfers between devices with their start and end apart: 2, of which 1 were waited for; matrix products, arithmetic and copies ran while one was open for 0% of the time, Pallas kernels for 0%

commit v1 on v0

--- a/solution.py
+++ b/solution.py
@@ -61,21 +61,18 @@
 
 
 def local(wannier_g, rp_coords, q_coords, k_index, k_vectors, kq_vectors, modes):
-    q_all = lax.all_gather(q_coords, ("rp", "pb"), axis=1, tiled=True)
-    total = q_all.shape[1]
-    groups = lax.axis_size("rp")
-    block = total // groups
+    devices = lax.axis_size("rp") * lax.axis_size("pb")
+    per_device = q_coords.shape[1]
+    sent = jnp.broadcast_to(q_coords.T[None], (devices, per_device, 3))
+    q_all = lax.all_to_all(sent, ("rp", "pb"), split_axis=0, concat_axis=0, tiled=True)
+    total = devices * per_device
+    q_rows = q_all.reshape(total, 3).T
     moved = lax.all_to_all(wannier_g, "rp", split_axis=3, concat_axis=1, tiled=True)
     right = moved.reshape(2 * moved.shape[1], -1)
-    q_blocks = q_all.reshape(3, groups, block).transpose(1, 0, 2)
-
-    def fourier_block(q_rows):
-        left_real, left_imag = phases(q_rows, rp_coords)
-        f_real = jnp.dot(left_real, right, preferred_element_type=jnp.float32).astype(jnp.bfloat16)
-        f_imag = jnp.dot(left_imag, right, preferred_element_type=jnp.float32).astype(jnp.bfloat16)
-        return jnp.stack([f_real, f_imag], 1)
-
-    fourier = lax.map(fourier_block, q_blocks).reshape(total, 2, moved.shape[2], moved.shape[3])
+    left_real, left_imag = phases(q_rows, rp_coords)
+    f_real = jnp.dot(left_real, right, preferred_element_type=jnp.float32).astype(jnp.bfloat16)
+    f_imag = jnp.dot(left_imag, right, preferred_element_type=jnp.float32).astype(jnp.bfloat16)
+    fourier = jnp.stack([f_real, f_imag], 1).reshape(total, 2, moved.shape[2], moved.shape[3])
     owned = one_exchange(fourier, ("rp", "pb"), ("rp", "pb"), (0, 0), (3, 2))
     select = (jnp.arange(k_vectors.shape[0]) == k_index[0]).astype(jnp.bfloat16)
     unit = jnp.einsum("k,kcnj->cnj", select, k_vectors, preferred_element_type=jnp.float32).astype(

time: 424 us -> 97.2 us (0.23)
  blocking collectives: 351 us -> 0 us
  starting transfers between devices: 11.5 us -> 27.2 us
  waiting for transfers between devices: 20.4 us -> 30.4 us
    all_gather x1 -> x0, blocking collectives: 351 us -> none  [local(): q_all = lax.all_gather(q_coords, ('rp', 'pb'), axis=1, tiled=True)]
    all_to_all x0 -> x1, starting transfers between devices: none -> 15.6 us  [local(): lax.all_to_all(sent, ('rp', 'pb'), split_axis=0, concat_axis=0, tiled=True)]
    all_to_all x0 -> x1, waiting for transfers between devices: none -> 9.9 us  [local(): lax.all_to_all(sent, ('rp', 'pb'), split_axis=0, concat_axis=0, tiled=True)]
    dynamic_update_slice x8 -> x0, local copies, waits for them, and re-layouts: 5.54 us -> none  [local(): lax.map(fourier_block, q_blocks)]
    neg x8 -> x1, other arithmetic: 7.76 us -> 8.51 us  [phases(): -sine]
  transfers between devices with their start and end apart: 2 -> 3, of which waited for: 1 -> 2; matrix products, arithmetic and copies ran while one was open for 0% -> 23% of each run, Pallas kernels for 0% -> 0%
where the time goes in v1:
time: 97.2 us; the launch traced here: 96.7 us
  waiting for transfers between devices  30.4 us (31%)
  starting transfers between devices  27.2 us (28%)
  other arithmetic  17.9 us (18%)
  local copies, waits for them, and re-layouts  15.9 us (16%)
  matrix products  4.57 us (5%)
    all_to_all x1, waiting for transfers between devices, one_exchange(): parts = lax.all_to_all(parts, axis, split_axis=0, concat_axis=0, tiled=True)  20.5 us
    all_to_all x1, starting transfers between devices, local(): lax.all_to_all(sent, ('rp', 'pb'), split_axis=0, concat_axis=0, tiled=True)  15.6 us
    all_to_all x1, waiting for transfers between devices, local(): lax.all_to_all(sent, ('rp', 'pb'), split_axis=0, concat_axis=0, tiled=True)  9.9 us
    neg x1, other arithmetic, phases(): -sine  8.51 us
    all_to_all x1, starting transfers between devices, one_exchange(): parts = lax.all_to_all(parts, axis, split_axis=0, concat_axis=0, tiled=True)  7.98 us
    convert_element_type x1, other arithmetic, phases(): cosine = jnp.cos(angle).astype(jnp.bfloat16)  7.68 us
    all_to_all x1, starting transfers between devices, local(): lax.all_to_all(wannier_g, 'rp', split_axis=3, concat_axis=1, tiled=True)  3.54 us
    unnamed x8, local copies, waits for them, and re-layouts  3.16 us
  transfers between devices with their start and end apart: 3, of which 2 were waited for; matrix products, arithmetic and copies ran while one was open for 23% of the time, Pallas kernels for 0%

profile of v1, /device:TPU:1, one launch (start us, length us, event | category | flops | bytes accessed | tf_op | source)
XLA Modules:
  0.0 96.7 jit_solution(9889160449902464923)
XLA Ops:
  0.0 1.5 %broadcast_in_dim.2 = s32[256,2,3]{2,1,0:T(2,128)} broadcast(s32[2,3]{1,0:T(2,128)} %bitcast.120), dimensions={1,2} | broadcast | bytes 6168 | tf_op jit(solution)/shard_map/broadcast_in_dim | solution.py:66
  1.5 15.6 %all-to-all-start = ((s32[256,2,3]{2,1,0:T(2,128)}), s32[256,2,3]{2,1,0:T(2,128)S(1)}, u32[]{:S(2)}, u32[]{:S(2)}) async-start(s32[256,2,3]{2,1,0:T(2,128)} %broadcast_in_dim.2), calls=%async_computation | async-start | bytes 524288 | tf_op jit(solution)/shard_map/all_to_all | solution.py:67
  17.1 0.9 fusion.41
  18.7 0.2 fusion.23
  19.0 0.7 fusion.42
  19.9 3.0 %copy.118 = bf16[2,128,1,1152]{1,0,2,3:T(2,128)(2,1)} copy(bf16[2,128,1,1152]{3,1,2,0:T(8,128)(2,1)} %param.7) | data formatting | bytes 1179648 | tf_op args[0]
  22.8 9.9 %all-to-all-done = s32[256,2,3]{2,1,0:T(2,128)S(1)} async-done(((s32[256,2,3]{2,1,0:T(2,128)}), s32[256,2,3]{2,1,0:T(2,128)S(1)}, u32[]{:S(2)}, u32[]{:S(2)}) %all-to-all-start) | async-done | bytes 6176 | tf_op jit(solution)/shard_map/all_to_all | solution.py:67
  32.7 3.5 %all-to-all-start.1 = ((bf16[2,128,1,1152]{1,0,2,3:T(2,128)(2,1)}), bf16[2,128,1,1152]{1,0,2,3:T(2,128)(2,1)S(1)}, u32[]{:S(2)}, u32[]{:S(2)}) async-start(bf16[2,128,1,1152]{1,0,2,3:T(2,128)(2,1)} %copy.118), calls=%async_computation.1 | async-start | bytes 1179648 | tf_op jit(solution)/shard_map/all_to_all | solution.py:70
  36.4 0.5 multiply_reduce_fusion
  36.9 7.7 %cosine_convert_fusion = bf16[512,1024]{1,0:T(8,128)(2,1)S(1)} fusion(s32[512,1024]{1,0:T(8,128)S(1)} %multiply_reduce_fusion), kind=kLoop, calls=%fused_computation.18 | loop fusion | flops 7340032 | bytes 3145728 | tf_op jit(solution)/shard_map/convert_element_type | solution.py:37
  44.6 8.5 %fusion.40 = (bf16[512,1024]{1,0:T(8,128)(2,1)}, bf16[512,1024]{1,0:T(8,128)(2,1)S(1)}) fusion(s32[512,1024]{1,0:T(8,128)S(1)} %multiply_reduce_fusion), kind=kLoop, calls=%fused_computation.62 | loop fusion | flops 8912896 | bytes 4194304 | tf_op jit(solution)/shard_map/neg | solution.py:39
  53.2 0.2 copy.120
  53.4 0.3 reshape.54
  53.6 2.1 %fusion.16 = bf16[512,144]{0,1:T(8,128)(2,1)S(1)} fusion(bf16[2048,144]{0,1:T(8,128)(2,1)S(1)} %reshape.54, bf16[512,1024]{1,0:T(8,128)(2,1)} %get-tuple-element.7, bf16[512,1024]{1,0:T(8,128)(2,1)S(1)} %cosine_convert_fusion), kind=kOutput, calls=%fused_computation.23 | convolution fusion | flops 306257920 | bytes 2834432 | tf_op jit(solution)/shard_map/dot_general | solution.py:73
  55.7 0.1 copy.121
  55.8 0.1 stack.72
  56.0 0.8 fusion.13
  56.8 0.1 copy.122
  57.0 0.1 stack.73
  57.1 0.8 pad_maximum_fusion
  58.0 1.2 %copy.123 = bf16[256,2,2,1,144]{4,1,3,2,0:T(2,128)(2,1)} copy(bf16[256,2,2,1,144]{4,1,0,3,2:T(2,128)(2,1)S(1)} %pad_maximum_fusion) | data formatting | bytes 589824 | tf_op jit(solution)/shard_map/stack | solution.py:75
  59.1 8.0 %all-to-all-start.2 = ((bf16[256,2,2,1,144]{4,1,3,2,0:T(2,128)(2,1)}), bf16[256,2,2,1,144]{4,1,3,2,0:T(2,128)(2,1)S(1)}, u32[]{:S(2)}, u32[]{:S(2)}) async-start(bf16[256,2,2,1,144]{4,1,3,2,0:T(2,128)(2,1)} %copy.123), calls=%async_computation.2 | async-start | bytes 1048576 | tf_op jit(solution)/shard_map/all_to_all | solution.py:29
  67.4 0.1 maximum_bitcast_fusion
  67.6 20.5 %all-to-all-done.2 = bf16[256,2,2,1,144]{4,1,3,2,0:T(2,128)(2,1)S(1)} async-done(((bf16[256,2,2,1,144]{4,1,3,2,0:T(2,128)(2,1)}), bf16[256,2,2,1,144]{4,1,3,2,0:T(2,128)(2,1)S(1)}, u32[]{:S(2)}, u32[]{:S(2)}) %all-to-all-start.2) | async-done | bytes 294944 | tf_op jit(solution)/shard_map/all_to_all | solution.py:29
  88.0 0.3 copy.167
  88.3 0.5 reshape.56
  88.8 2.8 %reshape_reshape.3 = bf16[2,2,32,32,36]{4,3,2,1,0:T(8,128)(2,1)S(1)} reshape(bf16[2,2,32,1,1152]{4,2,1,0,3:T(8,128)(2,1)S(1)} %bitcast.112) | data formatting | bytes 589824 | tf_op jit(solution)/shard_map/reshape;reshape | solution.py:46
  91.6 0.5 fusion.11
  92.1 0.5 fusion.12
  92.6 0.5 convolution_bitcast_fusion
  93.1 1.2 %copy.129 = f32[2,2,32,32,36]{4,3,2,1,0:T(8,128)S(1)} copy(f32[2,2,32,32,36]{4,2,3,1,0:T(8,128)S(1)} %convolution_bitcast_fusion) | data formatting | bytes 1179648 | tf_op jit(solution)/shard_map/qcmju,qcmdi->qdiju/dot_general | solution.py:59
  94.3 2.4 %reshape.57 = f32[2,2,32,1152]{3,2,1,0:T(8,128)} reshape(f32[2,2,32,32,36]{4,3,2,1,0:T(8,128)S(1)} %copy.129) | data formatting | bytes 1179648 | tf_op jit(solution)/shard_map/reshape | solution.py:60
  (18 shorter events, 0.7 us)
Async XLA Ops:
  0.0 18.7 %copy-start = (bf16[8,2,32,32]{3,2,1,0:T(8,128)(2,1)S(1)}, bf16[8,2,32,32]{3,2,1,0:T(8,128)(2,1)}, u32[]{:S(2)}) copy-start(bf16[8,2,32,32]{3,2,1,0:T(8,128)(2,1)} %param.11) | copy-start | bytes 98308
  0.0 36.4 %copy-start.1 = (s32[3,1024]{1,0:T(4,128)S(1)}, s32[3,1024]{1,0:T(4,128)}, u32[]{:S(2)}) copy-start(s32[3,1024]{1,0:T(4,128)} %param.8) | copy-start | bytes 36868
  1.5 31.2 %all-to-all-start = ((s32[256,2,3]{2,1,0:T(2,128)}), s32[256,2,3]{2,1,0:T(2,128)S(1)}, u32[]{:S(2)}, u32[]{:S(2)}) async-start(s32[256,2,3]{2,1,0:T(2,128)} %broadcast_in_dim.2), calls=%async_computation | async-start | bytes 524288 | tf_op jit(solution)/shard_map/all_to_all | solution.py:67
  32.7 20.4 %all-to-all-start.1 = ((bf16[2,128,1,1152]{1,0,2,3:T(2,128)(2,1)}), bf16[2,128,1,1152]{1,0,2,3:T(2,128)(2,1)S(1)}, u32[]{:S(2)}, u32[]{:S(2)}) async-start(bf16[2,128,1,1152]{1,0,2,3:T(2,128)(2,1)} %copy.118), calls=%async_computation.1 | async-start | bytes 1179648 | tf_op jit(solution)/shard_map/all_to_all | solution.py:70
  59.1 28.9 %all-to-all-start.2 = ((bf16[256,2,2,1,144]{4,1,3,2,0:T(2,128)(2,1)}), bf16[256,2,2,1,144]{4,1,3,2,0:T(2,128)(2,1)S(1)}, u32[]{:S(2)}, u32[]{:S(2)}) async-start(bf16[256,2,2,1,144]{4,1,3,2,0:T(2,128)(2,1)} %copy.123), calls=%async_computation.2 | async-start | bytes 1048576 | tf_op jit(solution)/shard_map/all_to_all | solution.py:29

commit v2 on v1

v2 whole, which is shorter than its diff:
```python
import math

import jax
import jax.numpy as jnp
import numpy as np
from jax import lax
from jax.experimental import pallas as pl
from jax.experimental.pallas import tpu as pltpu
from jax.sharding import PartitionSpec as P

NK = 16
LANES = 128
EXTRA = 16
BANDS = 32
BRANCHES = 36
SLOT = 64
AXES = ("rp", "pb")


def sine_series():
    points = np.arange(1, 5) / NK
    powers = np.stack([points ** (2 * k) for k in range(4)], 1)
    values = np.sin(2 * math.pi * points) / points
    return [float(c) for c in np.linalg.solve(powers, values)]


SERIES = sine_series()


def lane_of(shape):
    return lax.broadcasted_iota(jnp.int32, shape, len(shape) - 1)


def turned(x, shift):
    shift %= LANES
    return pltpu.roll(x, shift, 1) if shift else x


def pack_kernel(w_ref, o_ref):
    groups = o_ref.shape[0]
    rows = w_ref.shape[0]
    cut = rows * EXTRA // LANES
    pieces = rows // cut
    for a in range(groups):
        o_ref[a, :rows, :] = w_ref[:, a * LANES : (a + 1) * LANES]
        o_ref[a, rows + cut :, :] = jnp.zeros((o_ref.shape[1] - rows - cut, LANES), o_ref.dtype)
    tail = w_ref[:, groups * LANES :].astype(jnp.float32)
    lane = lane_of((cut, LANES))
    half = pieces // 2
    for a in range(groups):
        mixed = jnp.zeros((cut, LANES), jnp.float32)
        for j in range(pieces):
            place = 2 * (j % half) + j // half
            piece = turned(tail[j * cut : (j + 1) * cut], EXTRA * (place - a))
            mixed = jnp.where(lane // EXTRA == place, piece, mixed)
        o_ref[a, rows : rows + cut, :] = mixed.astype(o_ref.dtype)


def wave(u):
    w = 0.25 - jnp.abs(u - jnp.round(u))
    s = w * w
    value = SERIES[3]
    for c in SERIES[2::-1]:
        value = value * s + c
    return value * w


def fourier_kernel(x_ref, r_ref, o_ref, left, right):
    groups = x_ref.shape[0]
    span = r_ref.shape[1] // groups
    vectors = groups * span
    rows = 2 * span
    cut = rows * EXTRA // LANES
    half = span // cut
    lane = lane_of((cut, LANES))
    per_group = left.shape[0] // groups
    r_all = r_ref[...]
    for a in range(groups):
        coords = x_ref[a, rows + cut :, :].astype(jnp.float32)
        q_rows = coords.T[:per_group].astype(jnp.bfloat16)
        turns = jnp.dot(q_rows, r_all, preferred_element_type=jnp.float32)
        at = slice(a * per_group, (a + 1) * per_group)
        left[at, :vectors] = wave(turns).astype(jnp.bfloat16)
        left[at, vectors:] = wave(turns - 0.25).astype(jnp.bfloat16)
    for a in range(groups):
        real = x_ref[a, :span, :]
        imag = x_ref[a, span:rows, :]
        top = a * span
        low = vectors + a * span
        right[top : top + span, :LANES] = real
        right[top : top + span, LANES : 2 * LANES] = imag
        right[low : low + span, :LANES] = -imag
        right[low : low + span, LANES : 2 * LANES] = real
        mixed = x_ref[a, rows : rows + cut, :].astype(jnp.float32)
        for j in range(half):
            first = turned(mixed, -2 * EXTRA * j)
            second = jnp.where(lane < EXTRA, -turned(first, -EXTRA), turned(first, EXTRA))
            right[top + j * cut : top + (j + 1) * cut, 2 * LANES :] = first.astype(jnp.bfloat16)
            right[low + j * cut : low + (j + 1) * cut, 2 * LANES :] = second.astype(jnp.bfloat16)
    total = jnp.dot(left[...], right[...], preferred_element_type=jnp.float32)
    for k in range(3):
        part = total[:, k * LANES : (k + 1) * LANES].astype(jnp.bfloat16)
        o_ref[:, k] = part.reshape(o_ref.shape[0], 2, LANES)


def rotate_kernel(x_ref, v_ref, e_ref, u_ref, o_ref, spread, mixed):
    groups = x_ref.shape[0]
    pairs = 2 * BANDS
    lane = lane_of((pairs, LANES))
    tiles = []
    for a in range(groups):
        tiles.append(jnp.concatenate([x_ref[a, 0], x_ref[a, 1]], 0))
    tails = [x_ref[a, 2].astype(jnp.float32) for a in range(groups)]
    parts = []
    for c in range(2):
        part = jnp.zeros((pairs, LANES), jnp.float32)
        for a in range(groups):
            part = jnp.where(lane // EXTRA == a, turned(tails[a], EXTRA * (a - c)), part)
        parts.append(part.astype(jnp.bfloat16))
    tiles.append(jnp.concatenate(parts, 0))
    field = [jnp.dot(v_ref[...], t, preferred_element_type=jnp.float32) for t in tiles]

    lane = lane_of((BANDS, LANES))
    for q in range(2):
        for n in range(BANDS):
            t, s = divmod(BRANCHES * n, LANES)
            halves = []
            for c in range(2):
                at = slice((2 * q + c) * BANDS, (2 * q + c + 1) * BANDS)
                piece = field[t][at]
                if s + BRANCHES > LANES:
                    piece = jnp.where(lane >= s, piece, field[t + 1][at])
                halves.append(turned(piece, SLOT * c - s))
            spread[q, pl.ds(n, BANDS, stride=BANDS), :] = jnp.where(lane < SLOT, halves[0], halves[1])

    modes_done = [
        jnp.dot(spread[q].astype(jnp.bfloat16), e_ref[q], preferred_element_type=jnp.float32).astype(
            jnp.bfloat16
        )
        for q in range(2)
    ]
    block = u_ref.shape[1]
    for g in range(BANDS * BANDS // block):
        at = slice(g * block, (g + 1) * block)
        plain = jnp.concatenate([modes_done[0][at, :LANES], modes_done[1][at, :LANES]], 1)
        turned_by_i = jnp.concatenate([modes_done[0][at, LANES:], modes_done[1][at, LANES:]], 1)
        done = jnp.dot(u_ref[0], plain, preferred_element_type=jnp.float32) + jnp.dot(
            u_ref[1], turned_by_i, preferred_element_type=jnp.float32
        )
        for q in range(2):
            mixed[q, at, :] = done[:, q * LANES : (q + 1) * LANES]

    for q in range(2):
        for c in range(2):
            out = None
            for j in range(BANDS):
                t, s = divmod(BRANCHES * j, LANES)
                piece = mixed[q, pl.ds(j, BANDS, stride=BANDS), :]
                piece = turned(piece, s - SLOT * c)
                out = piece if out is None else jnp.where(lane >= s, piece, out)
                if s + BRANCHES >= LANES:
                    o_ref[q, c, :, t * LANES : (t + 1) * LANES] = out
                    out = piece if s + BRANCHES > LANES else None


def room(mib):
    return pltpu.CompilerParams(vmem_limit_bytes=mib * 2**20)


def vmem(shape, dtype):
    return jax.ShapeDtypeStruct(shape, dtype)


def complex_block(real, imag):
    return jnp.stack([jnp.stack([real, imag], 1), jnp.stack([-imag, real], 1)], 0)


def local(wannier_g, rp_coords, q_coords, k_index, k_vectors, kq_vectors, modes):
    groups = lax.axis_size("rp")
    columns = lax.axis_size("pb")
    devices = groups * columns
    per_device = q_coords.shape[1]
    span = wannier_g.shape[1]
    rows = 2 * span
    cut = rows * EXTRA // LANES
    chunk = rows + cut + 8

    with jax.named_scope("coords"):
        sent = jnp.broadcast_to(q_coords.astype(jnp.bfloat16)[None], (columns, 3, per_device))
        near = lax.all_to_all(sent, "pb", split_axis=0, concat_axis=0, tiled=True)
        near = near.transpose(1, 0, 2).reshape(3, columns * per_device)
        near = jnp.pad(near, ((0, 5), (0, LANES - columns * per_device)))
    with jax.named_scope("pack"):
        packed = pl.pallas_call(
            pack_kernel,
            out_shape=vmem((groups, chunk, LANES), jnp.bfloat16),
            compiler_params=room(8),
            name="pack",
        )(wannier_g.reshape(rows, wannier_g.shape[3]))
        packed = packed.at[:, rows + cut :, :].set(jnp.broadcast_to(near, (groups, 8, LANES)))
    with jax.named_scope("wannier"):
        moved = lax.all_to_all(packed, "rp", split_axis=0, concat_axis=0, tiled=True)

    turns_of = jnp.pad(rp_coords.astype(jnp.float32) / NK, ((0, 5), (0, 0))).astype(jnp.bfloat16)
    vectors = rp_coords.shape[1]
    total = devices * per_device
    with jax.named_scope("fourier"):
        fourier = pl.pallas_call(
            fourier_kernel,
            out_shape=vmem((devices, 3, per_device, LANES), jnp.bfloat16),
            scratch_shapes=[
                pltpu.VMEM((total, 2 * vectors), jnp.bfloat16),
                pltpu.VMEM((2 * vectors, 3 * LANES), jnp.bfloat16),
            ],
            compiler_params=room(16),
            name="fourier",
        )(moved, turns_of)
    with jax.named_scope("owners"):
        owned = lax.all_to_all(fourier, AXES, split_axis=0, concat_axis=0, tiled=True)
        owned = owned.reshape(groups, columns, 3, per_device, LANES).transpose(0, 2, 1, 3, 4)
        owned = owned.reshape(groups, 3, columns * per_device, LANES)

    with jax.named_scope("tables"):
        select = (jnp.arange(k_vectors.shape[0]) == k_index[0]).astype(jnp.bfloat16)
        unit = jnp.einsum("k,kcnj->cnj", select, k_vectors, preferred_element_type=jnp.float32)
        eight = jnp.eye(8, dtype=jnp.float32)
        u_table = jnp.einsum("ab,cnj->cajbn", eight, unit).reshape(2, 8 * BANDS, 8 * BANDS)
        u_table = u_table.astype(jnp.bfloat16)
        v_real, v_imag = kq_vectors[:, 0], kq_vectors[:, 1]
        v_block = jnp.stack([jnp.stack([v_real, -v_imag], 2), jnp.stack([v_imag, v_real], 2)], 1)
        own = jnp.eye(per_device, dtype=jnp.bfloat16)
        v_table = v_block.transpose(0, 3, 4, 1, 2)[..., None] * own[:, None, None, None, None, :]
        v_table = v_table.reshape(per_device * 2 * BANDS, 2 * BANDS * per_device)
        rest = SLOT - BRANCHES
        e_pad = jnp.pad(modes, ((0, 0), (0, 0), (0, rest), (0, rest)))
        e_real, e_imag = e_pad[:, 0], e_pad[:, 1]
        e_table = jnp.concatenate(
            [
                jnp.concatenate([e_real, e_imag, -e_imag, e_real], 2),
                jnp.concatenate([-e_imag, e_real, -e_real, -e_imag], 2),
            ],
            1,
        )
    with jax.named_scope("rotate"):
        return pl.pallas_call(
            rotate_kernel,
            out_shape=vmem((per_device, 2, BANDS, BANDS * BRANCHES), jnp.float32),
            scratch_shapes=[
                pltpu.VMEM((per_device, BANDS * BANDS, LANES), jnp.float32),
                pltpu.VMEM((per_device, BANDS * BANDS, LANES), jnp.float32),
            ],
            compiler_params=room(16),
            name="rotate",
        )(owned, v_table, e_table, u_table)


def solution(mesh):
    return jax.shard_map(
        local,
        mesh=mesh,
        in_specs=(
            P(None, "rp", "pb", None),
            P(),
            P(None, AXES),
            P(),
            P(),
            P(AXES, None, None, None),
            P(AXES, None, None, None),
        ),
        out_specs=P(AXES, None, None, None),
        check_vma=False,
    )
```

time: 97.2 us -> 71.4 us (0.73)
  other arithmetic: 17.9 us -> 1.37 us
  local copies, waits for them, and re-layouts: 15.9 us -> 3.92 us
  Pallas kernels: 0 us -> 7.81 us
  matrix products: 4.57 us -> 0.19 us
  starting transfers between devices: 27.2 us -> 24.2 us
  waiting for transfers between devices: 30.4 us -> 32.7 us
    neg x4 -> x2, other arithmetic: 8.56 us -> 0.02 us  [the longest x1 0.02 us: local(): -e_real]
    pallas_call x0 -> x3, Pallas kernels: none -> 7.81 us  [the longest x1 3.52 us: local(): pl.pallas_call(fourier_kernel, out_shape=vmem((devices, 3, per_device, LA...]
    convert_element_type x1 -> x3, other arithmetic: 7.68 us -> 1.01 us  [the longest x1 0.72 us: local(): q_coords.astype(jnp.bfloat16)[None]]
    dot_general x5 -> x0, matrix products: 4.38 us -> none  [the longest x1 2.06 us: local(): jnp.dot(left_real, right, preferred_element_type=jnp.float32)]
    another operation x5 -> x0, local copies, waits for them, and re-layouts: 4.24 us -> none  [the longest x1 2.8 us: rotate(): field = fourier.reshape(count, 2, bands, bands, branches)]
    reshape x5 -> x2, local copies, waits for them, and re-layouts: 3.54 us -> 0.48 us  [the longest x1 0.4 us: local(): owned.reshape(groups, columns, 3, per_device, LANES)]
    all_to_all x3, starting transfers between devices: 27.2 us -> 24.2 us  [the longest x1 12.7 us: local(): near = lax.all_to_all(sent, 'pb', split_axis=0, concat_axis=0, tiled=True)]
    all_to_all x3, waiting for transfers between devices: 30.4 us -> 32.7 us  [the longest x1 16.6 us: local(): lax.all_to_all(fourier, AXES, split_axis=0, concat_axis=0, tiled=True)]
  transfers between devices with their start and end apart: 3 -> 3, of which waited for: 2 -> 3; matrix products, arithmetic and copies ran while one was open for 23% -> 3% of each run, Pallas kernels for 0% -> 1%
where the time goes in v2:
time: 71.4 us; the launch traced here: 71.1 us
  waiting for transfers between devices  32.7 us (46%)
  starting transfers between devices  24.2 us (34%)
  Pallas kernels  7.81 us (11%)
  local copies, waits for them, and re-layouts  3.92 us (5%)
  other arithmetic  1.37 us (2%)
  between operations  0.85 us (1%)
    all_to_all x1, waiting for transfers between devices, local(): lax.all_to_all(fourier, AXES, split_axis=0, concat_axis=0, tiled=True)  16.6 us
    all_to_all x1, starting transfers between devices, local(): near = lax.all_to_all(sent, 'pb', split_axis=0, concat_axis=0, tiled=True)  12.7 us
    all_to_all x1, waiting for transfers between devices, local(): lax.all_to_all(packed, 'rp', split_axis=0, concat_axis=0, tiled=True)  8.9 us
    all_to_all x1, waiting for transfers between devices, local(): near = lax.all_to_all(sent, 'pb', split_axis=0, concat_axis=0, tiled=True)  7.23 us
    all_to_all x1, starting transfers between devices, local(): lax.all_to_all(fourier, AXES, split_axis=0, concat_axis=0, tiled=True)  6.99 us
    all_to_all x1, starting transfers between devices, local(): lax.all_to_all(packed, 'rp', split_axis=0, concat_axis=0, tiled=True)  4.44 us
    pallas_call x1, Pallas kernels, local(): pl.pallas_call(fourier_kernel, out_shape=vmem((devices, 3, per_device, LA...  3.52 us
    pallas_call x1, Pallas kernels, local(): pl.pallas_call(rotate_kernel, out_shape=vmem((per_device, 2, BANDS, BANDS...  3.25 us
  transfers between devices with their start and end apart: 3, of which 3 were waited for; matrix products, arithmetic and copies ran while one was open for 3% of the time, Pallas kernels for 1%

profile of v2, /device:TPU:1, one launch (start us, length us, event | category | flops | bytes accessed | tf_op | source)
XLA Modules:
  0.0 71.1 jit_solution(14917430538228273258)
XLA Ops:
  0.0 0.0 copy-start
  0.0 0.7 %convert_element_type.29 = bf16[3,2]{0,1:T(2,128)(2,1)S(1)} convert(s32[3,2]{0,1:T(2,128)} %param.11) | non-fusion elementwise | flops 6 | bytes 36 | tf_op jit(solution)/shard_map/coords/convert_element_type | solution.py:189
  0.7 0.6 broadcast_in_dim.2
  1.3 12.7 %all-to-all-start = ((bf16[32,3,2]{1,2,0:T(2,128)(2,1)}), bf16[32,3,2]{1,2,0:T(2,128)(2,1)S(1)}, u32[]{:S(2)}, u32[]{:S(2)}) async-start(bf16[32,3,2]{1,2,0:T(2,128)(2,1)} %broadcast_in_dim.2), calls=%async_computation | async-start | bytes 32768 | tf_op jit(solution)/shard_map/coords/all_to_all | solution.py:190
  14.1 0.0 copy-start.1
  14.1 1.1 %copy-done.1 = bf16[2,128,1,1152]{3,1,2,0:T(8,128)(2,1)S(1)} copy-done((bf16[2,128,1,1152]{3,1,2,0:T(8,128)(2,1)S(1)}, bf16[2,128,1,1152]{3,1,2,0:T(8,128)(2,1)}, u32[]{:S(2)}) %copy-start.1) | copy-done | bytes 589848
  15.2 0.0 copy-start.4
  15.2 1.0 %pack.1 = bf16[8,296,128]{2,1,0:T(8,128)(2,1)} custom-call(bf16[256,1152]{1,0:T(8,128)(2,1)S(1)} %bitcast.45), custom_call_target="tpu_custom_call" | custom-call | tf_op jit(solution)/shard_map/pack/pack/pallas_call | solution.py:194
  16.2 7.2 %all-to-all-done = bf16[32,3,2]{1,2,0:T(2,128)(2,1)S(1)} async-done(((bf16[32,3,2]{1,2,0:T(2,128)(2,1)}), bf16[32,3,2]{1,2,0:T(2,128)(2,1)S(1)}, u32[]{:S(2)}, u32[]{:S(2)}) %all-to-all-start) | async-done | bytes 416 | tf_op jit(solution)/shard_map/coords/all_to_all | solution.py:190
  23.4 0.1 copy.28
  23.5 0.6 broadcast_dynamic-update-slice_fusion
  24.1 4.4 %all-to-all-start.1 = ((bf16[8,296,128]{2,1,0:T(8,128)(2,1)}), bf16[8,296,128]{2,1,0:T(8,128)(2,1)S(1)}, u32[]{:S(2)}, u32[]{:S(2)}) async-start(bf16[8,296,128]{2,1,0:T(8,128)(2,1)} %broadcast_dynamic-update-slice_fusion), calls=%async_computation.1 | async-start | bytes 1212416 | tf_op jit(solution)/shard_map/wannier/all_to_all | solution.py:202
  28.6 0.0 copy-done.4
  29.3 0.0 copy-done.2
  29.3 0.1 copy.22
  29.4 0.2 broadcast_multiply_fusion
  29.6 0.0 copy-start.3
  29.6 8.9 %all-to-all-done.1.x_ref = bf16[8,296,128]{2,1,0:T(8,128)(2,1)S(1)} async-done(((bf16[8,296,128]{2,1,0:T(8,128)(2,1)}), bf16[8,296,128]{2,1,0:T(8,128)(2,1)S(1)}, u32[]{:S(2)}, u32[]{:S(2)}) %all-to-all-start.1) | async-done | bytes 606240 | tf_op jit(solution)/shard_map/wannier/all_to_all | solution.py:202
  38.5 3.5 %fourier.1 = bf16[256,3,2,128]{3,2,1,0:T(2,128)(2,1)} custom-call(bf16[8,296,128]{2,1,0:T(8,128)(2,1)S(1)} %all-to-all-done.1.x_ref, bf16[8,1024]{1,0:T(8,128)(2,1)S(1)} %pad.16.r_ref), custom_call_target="tpu_custom_call" | custom-call | tf_op jit(solution)/shard_map/fourier/fourier/pallas_call | solution.py:208
  42.0 7.0 %all-to-all-start.2 = ((bf16[256,3,2,128]{3,2,1,0:T(2,128)(2,1)}), bf16[256,3,2,128]{3,2,1,0:T(2,128)(2,1)S(1)}, u32[]{:S(2)}, u32[]{:S(2)}) async-start(bf16[256,3,2,128]{3,2,1,0:T(2,128)(2,1)} %fourier.1), calls=%async_computation.2 | async-start | bytes 786432 | tf_op jit(solution)/shard_map/owners/all_to_all | solution.py:219
  49.0 0.0 copy-done
  49.1 0.2 fusion.1
  49.3 0.1 copy.27
  49.3 0.0 copy-done.3
  49.3 0.1 mul.20
  49.5 0.1 copy.24.v_ref
  49.6 0.3 fusion
  49.9 0.7 convert_element_type.34.u_ref
  50.7 0.1 maximum_maximum_fusion.e_ref
  50.8 16.6 %all-to-all-done.2 = bf16[256,3,2,128]{3,2,1,0:T(2,128)(2,1)S(1)} async-done(((bf16[256,3,2,128]{3,2,1,0:T(2,128)(2,1)}), bf16[256,3,2,128]{3,2,1,0:T(2,128)(2,1)S(1)}, u32[]{:S(2)}, u32[]{:S(2)}) %all-to-all-start.2) | async-done | bytes 393248 | tf_op jit(solution)/shard_map/owners/all_to_all | solution.py:219
  67.4 0.4 copy.20
  67.8 3.3 %rotate.1 = f32[2,2,32,1152]{3,2,1,0:T(8,128)} custom-call(bf16[8,3,64,128]{3,2,1,0:T(8,128)(2,1)S(1)} %bitcast.44, bf16[128,128]{1,0:T(8,128)(2,1)S(1)} %copy.24.v_ref, bf16[2,128,256]{2,1,0:T(8,128)(2,1)S(1)} %maximum_maximum_fusion.e_ref, bf16[2,256,256]{2,1,0:T(8,128)(2,1)S(1)} %convert_element_type.34.u_ref), custom_call_target="tpu_custom_call" | custom-call | tf_op jit(solution)/shard_map/rotate/rotate/pallas_call | solution.py:245
  (13 shorter events, 0.1 us)
Async XLA Ops:
  0.0 49.0 %copy-start = (bf16[8,2,32,32]{3,2,1,0:T(8,128)(2,1)S(1)}, bf16[8,2,32,32]{3,2,1,0:T(8,128)(2,1)}, u32[]{:S(2)}) copy-start(bf16[8,2,32,32]{3,2,1,0:T(8,128)(2,1)} %param.13) | copy-start | bytes 98308
  1.3 22.1 %all-to-all-start = ((bf16[32,3,2]{1,2,0:T(2,128)(2,1)}), bf16[32,3,2]{1,2,0:T(2,128)(2,1)S(1)}, u32[]{:S(2)}, u32[]{:S(2)}) async-start(bf16[32,3,2]{1,2,0:T(2,128)(2,1)} %broadcast_in_dim.2), calls=%async_computation | async-start | bytes 32768 | tf_op jit(solution)/shard_map/coords/all_to_all | solution.py:190
  14.1 1.1 %copy-start.1 = (bf16[2,128,1,1152]{3,1,2,0:T(8,128)(2,1)S(1)}, bf16[2,128,1,1152]{3,1,2,0:T(8,128)(2,1)}, u32[]{:S(2)}) copy-start(bf16[2,128,1,1152]{3,1,2,0:T(8,128)(2,1)} %param.9) | copy-start | bytes 1769476
  15.2 13.4 %copy-start.4 = (s32[3,1024]{1,0:T(4,128)S(1)}, s32[3,1024]{1,0:T(4,128)}, u32[]{:S(2)}) copy-start(s32[3,1024]{1,0:T(4,128)} %param.10) | copy-start | bytes 36868
  15.2 14.1 %copy-start.2 = (bf16[2,2,32,32]{3,2,1,0:T(8,128)(2,1)S(1)}, bf16[2,2,32,32]{3,2,1,0:T(8,128)(2,1)}, u32[]{:S(2)}) copy-start(bf16[2,2,32,32]{3,2,1,0:T(8,128)(2,1)} %param.14) | copy-start | bytes 24580
  24.1 14.4 %all-to-all-start.1 = ((bf16[8,296,128]{2,1,0:T(8,128)(2,1)}), bf16[8,296,128]{2,1,0:T(8,128)(2,1)S(1)}, u32[]{:S(2)}, u32[]{:S(2)}) async-start(bf16[8,296,128]{2,1,0:T(8,128)(2,1)} %broadcast_dynamic-update-slice_fusion), calls=%async_computation.1 | async-start | bytes 1212416 | tf_op jit(solution)/shard_map/wannier/all_to_all | solution.py:202
  29.6 19.7 %copy-start.3 = (bf16[2,2,36,36]{3,1,2,0:T(2,128)(2,1)S(1)}, bf16[2,2,36,36]{3,1,2,0:T(2,128)(2,1)}, u32[]{:S(2)}) copy-start(bf16[2,2,36,36]{3,1,2,0:T(2,128)(2,1)} %param.15) | copy-start | bytes 31108
  42.0 25.4 %all-to-all-start.2 = ((bf16[256,3,2,128]{3,2,1,0:T(2,128)(2,1)}), bf16[256,3,2,128]{3,2,1,0:T(2,128)(2,1)S(1)}, u32[]{:S(2)}, u32[]{:S(2)}) async-start(bf16[256,3,2,128]{3,2,1,0:T(2,128)(2,1)} %fourier.1), calls=%async_computation.2 | async-start | bytes 786432 | tf_op jit(solution)/shard_map/owners/all_to_all | solution.py:219

commit v3 on v2

--- a/solution.py
+++ b/solution.py
@@ -109,8 +109,8 @@
     lane = lane_of((pairs, LANES))
     tiles = []
     for a in range(groups):
-        tiles.append(jnp.concatenate([x_ref[a, 0], x_ref[a, 1]], 0))
-    tails = [x_ref[a, 2].astype(jnp.float32) for a in range(groups)]
+        tiles.append(jnp.concatenate([x_ref[a, :, k].reshape(pairs, LANES) for k in range(2)], 0))
+    tails = [x_ref[a, :, 2].reshape(pairs, LANES).astype(jnp.float32) for a in range(groups)]
     parts = []
     for c in range(2):
         part = jnp.zeros((pairs, LANES), jnp.float32)
@@ -186,10 +186,10 @@
     chunk = rows + cut + 8
 
     with jax.named_scope("coords"):
-        sent = jnp.broadcast_to(q_coords.astype(jnp.bfloat16)[None], (columns, 3, per_device))
+        sent = jnp.broadcast_to(q_coords[None], (columns, 3, per_device))
         near = lax.all_to_all(sent, "pb", split_axis=0, concat_axis=0, tiled=True)
         near = near.transpose(1, 0, 2).reshape(3, columns * per_device)
-        near = jnp.pad(near, ((0, 5), (0, LANES - columns * per_device)))
+        near = jnp.pad(near.astype(jnp.bfloat16), ((0, 5), (0, LANES - columns * per_device)))
     with jax.named_scope("pack"):
         packed = pl.pallas_call(
             pack_kernel,
@@ -197,11 +197,42 @@
             compiler_params=room(8),
             name="pack",
         )(wannier_g.reshape(rows, wannier_g.shape[3]))
-        packed = packed.at[:, rows + cut :, :].set(jnp.broadcast_to(near, (groups, 8, LANES)))
+    near, rp_coords, k_index, k_vectors, kq_vectors, modes = lax.optimization_barrier(
+        (near, rp_coords, k_index, k_vectors, kq_vectors, modes)
+    )
+    turns_of = jnp.pad(rp_coords.astype(jnp.float32) / NK, ((0, 5), (0, 0))).astype(jnp.bfloat16)
+    with jax.named_scope("tables"):
+        select = (jnp.arange(k_vectors.shape[0]) == k_index[0]).astype(jnp.bfloat16)
+        unit = jnp.einsum("k,kcnj->cnj", select, k_vectors, preferred_element_type=jnp.float32)
+        eight = jnp.eye(8, dtype=jnp.float32)
+        u_table = jnp.einsum("ab,cnj->cajbn", eight, unit).reshape(2, 8 * BANDS, 8 * BANDS)
+        u_table = u_table.astype(jnp.bfloat16)
+        v_real, v_imag = kq_vectors[:, 0], kq_vectors[:, 1]
+        v_block = jnp.stack([jnp.stack([v_real, -v_imag], 2), jnp.stack([v_imag, v_real], 2)], 1)
+        twice = jnp.repeat(jnp.eye(2 * BANDS, dtype=jnp.bfloat16), per_device, 1)
+        v_table = jnp.einsum(
+            "qcmdi,cmk->qdik",
+            v_block,
+            twice.reshape(2, BANDS, 2 * BANDS * per_device),
+            preferred_element_type=jnp.float32,
+        ).reshape(per_device, 2 * BANDS, 2 * BANDS * per_device)
+        own = jnp.arange(2 * BANDS * per_device) % per_device == jnp.arange(per_device)[:, None]
+        v_table = jnp.where(own[:, None, :], v_table, 0.0).astype(jnp.bfloat16)
+        v_table = v_table.reshape(per_device * 2 * BANDS, 2 * BANDS * per_device)
+        rest = SLOT - BRANCHES
+        e_pad = jnp.pad(modes, ((0, 0), (0, 0), (0, rest), (0, rest)))
+        e_real, e_imag = e_pad[:, 0], e_pad[:, 1]
+        e_table = jnp.concatenate(
+            [
+                jnp.concatenate([e_real, e_imag, -e_imag, e_real], 2),
+                jnp.concatenate([-e_imag, e_real, -e_real, -e_imag], 2),
+            ],
+            1,
+        )
+    packed = packed.at[:, rows + cut :, :].set(jnp.broadcast_to(near, (groups, 8, LANES)))
     with jax.named_scope("wannier"):
         moved = lax.all_to_all(packed, "rp", split_axis=0, concat_axis=0, tiled=True)
 
-    turns_of = jnp.pad(rp_coords.astype(jnp.float32) / NK, ((0, 5), (0, 0))).astype(jnp.bfloat16)
     vectors = rp_coords.shape[1]
     total = devices * per_device
     with jax.named_scope("fourier"):
@@ -215,32 +246,13 @@
             compiler_params=room(16),
             name="fourier",
         )(moved, turns_of)
+    fourier, u_table, v_table, e_table = lax.optimization_barrier(
+        (fourier, u_table, v_table, e_table)
+    )
     with jax.named_scope("owners"):
         owned = lax.all_to_all(fourier, AXES, split_axis=0, concat_axis=0, tiled=True)
-        owned = owned.reshape(groups, columns, 3, per_device, LANES).transpose(0, 2, 1, 3, 4)
-        owned = owned.reshape(groups, 3, columns * per_device, LANES)
-
-    with jax.named_scope("tables"):
-        select = (jnp.arange(k_vectors.shape[0]) == k_index[0]).astype(jnp.bfloat16)
-        unit = jnp.einsum("k,kcnj->cnj", select, k_vectors, preferred_element_type=jnp.float32)
-        eight = jnp.eye(8, dtype=jnp.float32)
-        u_table = jnp.einsum("ab,cnj->cajbn", eight, unit).reshape(2, 8 * BANDS, 8 * BANDS)
-        u_table = u_table.astype(jnp.bfloat16)
-        v_real, v_imag = kq_vectors[:, 0], kq_vectors[:, 1]
-        v_block = jnp.stack([jnp.stack([v_real, -v_imag], 2), jnp.stack([v_imag, v_real], 2)], 1)
-        own = jnp.eye(per_device, dtype=jnp.bfloat16)
-        v_table = v_block.transpose(0, 3, 4, 1, 2)[..., None] * own[:, None, None, None, None, :]
-        v_table = v_table.reshape(per_device * 2 * BANDS, 2 * BANDS * per_device)
-        rest = SLOT - BRANCHES
-        e_pad = jnp.pad(modes, ((0, 0), (0, 0), (0, rest), (0, rest)))
-        e_real, e_imag = e_pad[:, 0], e_pad[:, 1]
-        e_table = jnp.concatenate(
-            [
-                jnp.concatenate([e_real, e_imag, -e_imag, e_real], 2),
-                jnp.concatenate([-e_imag, e_real, -e_real, -e_imag], 2),
-            ],
-            1,
-        )
+        owned = owned.reshape(groups, columns, 3, per_device, LANES)
+
     with jax.named_scope("rotate"):
         return pl.pallas_call(
             rotate_kernel,

time: 71.4 us -> 70.5 us (0.987)
  blocking collectives: 0 us -> 24.9 us
  waiting for transfers between devices: 32.7 us -> 14.8 us
  starting transfers between devices: 24.2 us -> 17.3 us
  other arithmetic: 1.37 us -> 0.51 us
    all_to_all x0 -> x1, blocking collectives: none -> 24.9 us  [local(): lax.all_to_all(fourier, AXES, split_axis=0, concat_axis=0, tiled=True)]
    all_to_all x1 -> x0, waiting for transfers between devices: 16.6 us -> none  [local(): lax.all_to_all(fourier, AXES, split_axis=0, concat_axis=0, tiled=True)]
    all_to_all x1 -> x0, starting transfers between devices: 6.99 us -> none  [local(): lax.all_to_all(fourier, AXES, split_axis=0, concat_axis=0, tiled=True)]
    all_to_all x1, waiting for transfers between devices: 8.9 us -> 8.13 us  [local(): lax.all_to_all(packed, 'rp', split_axis=0, concat_axis=0, tiled=True)]
    broadcast_in_dim x1 -> x2, local copies, waits for them, and re-layouts: 0.62 us -> 1.36 us  [the longest x1 1.34 us: local(): sent = jnp.broadcast_to(q_coords[None], (columns, 3, per_device))]
    pallas_call x1, Pallas kernels: 3.52 us -> 2.78 us  [local(): pl.pallas_call(fourier_kernel, out_shape=vmem((devices, 3, per_device, LA...]
  transfers between devices with their start and end apart: 3 -> 2, of which waited for: 3 -> 2; matrix products, arithmetic and copies ran while one was open for 3% -> 3% of each run, Pallas kernels for 1% -> 1%
where the time goes in v3:
time: 70.5 us; the launch traced here: 70.2 us
  blocking collectives  24.9 us (35%)
  starting transfers between devices  17.3 us (25%)
  waiting for transfers between devices  14.8 us (21%)
  Pallas kernels  7.13 us (10%)
  local copies, waits for them, and re-layouts  4.28 us (6%)
  between operations  0.87 us (1%)
    all_to_all x1, blocking collectives, local(): lax.all_to_all(fourier, AXES, split_axis=0, concat_axis=0, tiled=True)  24.9 us
    all_to_all x1, starting transfers between devices, local(): near = lax.all_to_all(sent, 'pb', split_axis=0, concat_axis=0, tiled=True)  12.7 us
    all_to_all x1, waiting for transfers between devices, local(): lax.all_to_all(packed, 'rp', split_axis=0, concat_axis=0, tiled=True)  8.13 us
    all_to_all x1, waiting for transfers between devices, local(): near = lax.all_to_all(sent, 'pb', split_axis=0, concat_axis=0, tiled=True)  6.69 us
    all_to_all x1, starting transfers between devices, local(): lax.all_to_all(packed, 'rp', split_axis=0, concat_axis=0, tiled=True)  4.57 us
    pallas_call x1, Pallas kernels, local(): pl.pallas_call(rotate_kernel, out_shape=vmem((per_device, 2, BANDS, BANDS...  3.31 us
    pallas_call x1, Pallas kernels, local(): pl.pallas_call(fourier_kernel, out_shape=vmem((devices, 3, per_device, LA...  2.78 us
  transfers between devices with their start and end apart: 2, of which 2 were waited for; matrix products, arithmetic and copies ran while one was open for 3% of the time, Pallas kernels for 1%

profile of v3, /device:TPU:1, one launch (start us, length us, event | category | flops | bytes accessed | tf_op | source)
XLA Modules:
  0.0 70.2 jit_solution(2643239747749935311)
XLA Ops:
  0.0 0.0 copy-start
  0.0 0.0 copy-start.2
  0.0 1.3 %broadcast_in_dim.16 = s32[32,3,2]{1,2,0:T(2,128)} broadcast(s32[3,2]{0,1:T(2,128)} %param.11), dimensions={1,2} | broadcast | bytes 792 | tf_op jit(solution)/shard_map/coords/broadcast_in_dim | solution.py:189
  1.3 12.7 %all-to-all-start = ((s32[32,3,2]{1,2,0:T(2,128)}), s32[32,3,2]{1,2,0:T(2,128)S(1)}, u32[]{:S(2)}, u32[]{:S(2)}) async-start(s32[32,3,2]{1,2,0:T(2,128)} %broadcast_in_dim.16), calls=%async_computation | async-start | bytes 65536 | tf_op jit(solution)/shard_map/coords/all_to_all | solution.py:190
  14.2 0.0 copy-start.1
  14.2 1.1 %copy-done.1 = bf16[2,128,1,1152]{3,1,2,0:T(8,128)(2,1)S(1)} copy-done((bf16[2,128,1,1152]{3,1,2,0:T(8,128)(2,1)S(1)}, bf16[2,128,1,1152]{3,1,2,0:T(8,128)(2,1)}, u32[]{:S(2)}) %copy-start.1) | copy-done | bytes 589848
  15.2 1.0 %pack.1 = bf16[8,296,128]{2,1,0:T(8,128)(2,1)} custom-call(bf16[256,1152]{1,0:T(8,128)(2,1)S(1)} %bitcast.54), custom_call_target="tpu_custom_call" | custom-call | tf_op jit(solution)/shard_map/pack/pack/pallas_call | solution.py:194
  16.9 0.1 reshape.85
  17.0 0.1 copy.20
  17.1 6.7 %all-to-all-done = s32[32,3,2]{1,2,0:T(2,128)S(1)} async-done(((s32[32,3,2]{1,2,0:T(2,128)}), s32[32,3,2]{1,2,0:T(2,128)S(1)}, u32[]{:S(2)}, u32[]{:S(2)}) %all-to-all-start) | async-done | bytes 800 | tf_op jit(solution)/shard_map/coords/all_to_all | solution.py:190
  23.8 0.1 copy.26
  23.9 0.0 copy-done.2
  24.0 0.6 broadcast_dynamic-update-slice_fusion
  24.5 0.0 copy-start.4
  24.5 4.6 %all-to-all-start.1 = ((bf16[8,296,128]{2,1,0:T(8,128)(2,1)}), bf16[8,296,128]{2,1,0:T(8,128)(2,1)S(1)}, u32[]{:S(2)}, u32[]{:S(2)}) async-start(bf16[8,296,128]{2,1,0:T(8,128)(2,1)} %broadcast_dynamic-update-slice_fusion), calls=%async_computation.1 | async-start | bytes 1212416 | tf_op jit(solution)/shard_map/wannier/all_to_all | solution.py:234
  29.1 0.0 copy-done
  29.1 0.2 fusion.3
  29.3 0.1 copy.24
  29.4 0.3 fusion.2
  29.7 0.0 copy-done.4
  29.7 0.0 copy-start.3
  29.7 0.7 %convert_element_type.42.u_ref = bf16[2,256,256]{2,1,0:T(8,128)(2,1)S(1)} reshape(bf16[2,8,32,8,32]{4,3,2,1,0:T(8,128)(2,1)S(1)} %fusion.2) | data formatting | bytes 524288 | tf_op jit(solution)/shard_map/tables/convert_element_type | solution.py:209
  30.5 0.1 copy.19
  30.6 0.1 dot_general.22
  30.7 0.0 copy-done.3
  30.8 0.1 maximum_maximum_fusion.e_ref
  30.9 0.2 fusion.1
  31.1 8.1 %all-to-all-done.1.x_ref = bf16[8,296,128]{2,1,0:T(8,128)(2,1)S(1)} async-done(((bf16[8,296,128]{2,1,0:T(8,128)(2,1)}), bf16[8,296,128]{2,1,0:T(8,128)(2,1)S(1)}, u32[]{:S(2)}, u32[]{:S(2)}) %all-to-all-start.1) | async-done | bytes 606240 | tf_op jit(solution)/shard_map/wannier/all_to_all | solution.py:234
  39.2 2.8 %fourier.1 = bf16[256,3,2,128]{3,2,1,0:T(2,128)(2,1)S(1)} custom-call(bf16[8,296,128]{2,1,0:T(8,128)(2,1)S(1)} %all-to-all-done.1.x_ref, bf16[8,1024]{1,0:T(8,128)(2,1)S(1)} %pad.16.r_ref), custom_call_target="tpu_custom_call" | custom-call | tf_op jit(solution)/shard_map/fourier/fourier/pallas_call | solution.py:239
  42.0 24.9 %all_to_all.15 = bf16[256,3,2,128]{3,2,1,0:T(2,128)(2,1)S(1)} all-to-all(bf16[256,3,2,128]{3,2,1,0:T(2,128)(2,1)S(1)} %fourier.1), channel_id=1, replica_groups=mesh['rp'=8,'pb'=32] {'rp','pb'}, dimensions={0} | all-to-all | bytes 786432 | tf_op jit(solution)/shard_map/owners/all_to_all | solution.py:253
  66.9 3.3 %rotate.1 = f32[2,2,32,1152]{3,2,1,0:T(8,128)} custom-call(bf16[8,32,3,2,128]{4,3,2,1,0:T(2,128)(2,1)S(1)} %bitcast.53, bf16[128,128]{1,0:T(8,128)(2,1)S(1)} %bitcast.55, bf16[2,128,256]{2,1,0:T(8,128)(2,1)S(1)} %maximum_maximum_fusion.e_ref, bf16[2,256,256]{2,1,0:T(8,128)(2,1)S(1)} %convert_element_type.42.u_ref), custom_call_target="tpu_custom_call" | custom-call | tf_op jit(solution)/shard_map/rotate/rotate/pallas_call | solution.py:257
  (17 shorter events, 0.2 us)
Async XLA Ops:
  0.0 29.1 %copy-start = (bf16[8,2,32,32]{3,2,1,0:T(8,128)(2,1)S(1)}, bf16[8,2,32,32]{3,2,1,0:T(8,128)(2,1)}, u32[]{:S(2)}) copy-start(bf16[8,2,32,32]{3,2,1,0:T(8,128)(2,1)} %param.13) | copy-start | bytes 98308
  0.0 23.9 %copy-start.2 = (bf16[2,2,32,32]{3,2,1,0:T(8,128)(2,1)S(1)}, bf16[2,2,32,32]{3,2,1,0:T(8,128)(2,1)}, u32[]{:S(2)}) copy-start(bf16[2,2,32,32]{3,2,1,0:T(8,128)(2,1)} %param.14) | copy-start | bytes 24580
  1.3 22.5 %all-to-all-start = ((s32[32,3,2]{1,2,0:T(2,128)}), s32[32,3,2]{1,2,0:T(2,128)S(1)}, u32[]{:S(2)}, u32[]{:S(2)}) async-start(s32[32,3,2]{1,2,0:T(2,128)} %broadcast_in_dim.16), calls=%async_computation | async-start | bytes 65536 | tf_op jit(solution)/shard_map/coords/all_to_all | solution.py:190
  14.2 1.1 %copy-start.1 = (bf16[2,128,1,1152]{3,1,2,0:T(8,128)(2,1)S(1)}, bf16[2,128,1,1152]{3,1,2,0:T(8,128)(2,1)}, u32[]{:S(2)}) copy-start(bf16[2,128,1,1152]{3,1,2,0:T(8,128)(2,1)} %param.9) | copy-start | bytes 1769476
  24.5 5.1 %copy-start.4 = (s32[3,1024]{1,0:T(4,128)S(1)}, s32[3,1024]{1,0:T(4,128)}, u32[]{:S(2)}) copy-start(s32[3,1024]{1,0:T(4,128)} %param.10) | copy-start | bytes 36868
  24.5 14.7 %all-to-all-start.1 = ((bf16[8,296,128]{2,1,0:T(8,128)(2,1)}), bf16[8,296,128]{2,1,0:T(8,128)(2,1)S(1)}, u32[]{:S(2)}, u32[]{:S(2)}) async-start(bf16[8,296,128]{2,1,0:T(8,128)(2,1)} %broadcast_dynamic-update-slice_fusion), calls=%async_computation.1 | async-start | bytes 1212416 | tf_op jit(solution)/shard_map/wannier/all_to_all | solution.py:234
  29.7 1.0 %copy-start.3 = (bf16[2,2,36,36]{3,1,2,0:T(2,128)(2,1)S(1)}, bf16[2,2,36,36]{3,1,2,0:T(2,128)(2,1)}, u32[]{:S(2)}) copy-start(bf16[2,2,36,36]{3,1,2,0:T(2,128)(2,1)} %param.15) | copy-start | bytes 31108

commit v4 on v3

v4 whole, which is shorter than its diff:
```python
import math

import jax
import jax.numpy as jnp
import numpy as np
from jax import lax
from jax.experimental import pallas as pl
from jax.experimental.pallas import tpu as pltpu
from jax.sharding import PartitionSpec as P


NK = 16
LANES = 128
EXTRA = 16
BANDS = 32
BRANCHES = 36
SLOT = 64
AXES = ("rp", "pb")


def sine_series():
    points = np.arange(1, 5) / NK
    powers = np.stack([points ** (2 * k) for k in range(4)], 1)
    values = np.sin(2 * math.pi * points) / points
    return [float(c) for c in np.linalg.solve(powers, values)]


SERIES = sine_series()


def lane_of(shape):
    return lax.broadcasted_iota(jnp.int32, shape, len(shape) - 1)


def turned(x, shift):
    shift %= LANES
    return pltpu.roll(x, shift, 1) if shift else x


def pack_kernel(w_ref, o_ref, tail_ref, cut_ref, sems):
    groups, cut, _ = cut_ref.shape
    rows = w_ref.shape[0]
    pieces = rows // cut
    fetch = pltpu.make_async_copy(w_ref.at[:, groups * LANES :], tail_ref, sems.at[groups])
    fetch.start()
    moves = [
        pltpu.make_async_copy(
            w_ref.at[:, a * LANES : (a + 1) * LANES], o_ref.at[a, :rows, :], sems.at[a]
        )
        for a in range(groups)
    ]
    for move in moves:
        move.start()
    fetch.wait()
    tail = tail_ref[...].astype(jnp.float32)
    lane = lane_of((cut, LANES))
    half = pieces // 2
    for a in range(groups):
        mixed = jnp.zeros((cut, LANES), jnp.float32)
        for j in range(pieces):
            place = 2 * (j % half) + j // half
            piece = turned(tail[j * cut : (j + 1) * cut], EXTRA * (place - a))
            mixed = jnp.where(lane // EXTRA == place, piece, mixed)
        cut_ref[a] = mixed.astype(o_ref.dtype)
    last = pltpu.make_async_copy(cut_ref, o_ref.at[:, rows : rows + cut, :], sems.at[groups + 1])
    last.start()
    for move in moves:
        move.wait()
    last.wait()


def wave(u):
    w = 0.25 - jnp.abs(u - jnp.round(u))
    s = w * w
    value = SERIES[3]
    for c in SERIES[2::-1]:
        value = value * s + c
    return value * w


def fourier_kernel(x_ref, r_ref, o_ref, left, right):
    groups = x_ref.shape[0]
    span = r_ref.shape[1] // groups
    vectors = groups * span
    rows = 2 * span
    cut = rows * EXTRA // LANES
    half = span // cut
    lane = lane_of((cut, LANES))
    per_group = left.shape[0] // groups
    r_all = r_ref[...]
    for a in range(groups):
        coords = x_ref[a, rows + cut :, :].astype(jnp.float32)
        q_rows = coords.T[:per_group].astype(jnp.bfloat16)
        turns = jnp.dot(q_rows, r_all, preferred_element_type=jnp.float32)
        at = slice(a * per_group, (a + 1) * per_group)
        left[at, :vectors] = wave(turns).astype(jnp.bfloat16)
        left[at, vectors:] = wave(turns - 0.25).astype(jnp.bfloat16)
    for a in range(groups):
        real = x_ref[a, :span, :]
        imag = x_ref[a, span:rows, :]
        top = a * span
        low = vectors + a * span
        right[top : top + span, :LANES] = real
        right[top : top + span, LANES : 2 * LANES] = imag
        right[low : low + span, :LANES] = -imag
        right[low : low + span, LANES : 2 * LANES] = real
        mixed = x_ref[a, rows : rows + cut, :].astype(jnp.float32)
        for j in range(half):
            first = turned(mixed, -2 * EXTRA * j)
            second = jnp.where(lane < EXTRA, -turned(first, -EXTRA), turned(first, EXTRA))
            right[top + j * cut : top + (j + 1) * cut, 2 * LANES :] = first.astype(jnp.bfloat16)
            right[low + j * cut : low + (j + 1) * cut, 2 * LANES :] = second.astype(jnp.bfloat16)
    total = jnp.dot(left[...], right[...], preferred_element_type=jnp.float32)
    for k in range(3):
        part = total[:, k * LANES : (k + 1) * LANES].astype(jnp.bfloat16)
        o_ref[:, k] = part.reshape(o_ref.shape[0], 2, LANES)


def rotate_kernel(x_ref, v_ref, e_ref, u_ref, o_ref, spread, mixed, ready, sems):
    groups = x_ref.shape[0]
    pairs = 2 * BANDS
    lane = lane_of((pairs, LANES))
    tiles = []
    for a in range(groups):
        tiles.append(jnp.concatenate([x_ref[a, :, k].reshape(pairs, LANES) for k in range(2)], 0))
    tails = [x_ref[a, :, 2].reshape(pairs, LANES).astype(jnp.float32) for a in range(groups)]
    parts = []
    for c in range(2):
        part = jnp.zeros((pairs, LANES), jnp.float32)
        for a in range(groups):
            part = jnp.where(lane // EXTRA == a, turned(tails[a], EXTRA * (a - c)), part)
        parts.append(part.astype(jnp.bfloat16))
    tiles.append(jnp.concatenate(parts, 0))
    field = [jnp.dot(v_ref[...], t, preferred_element_type=jnp.float32) for t in tiles]

    lane = lane_of((BANDS, LANES))
    modes_done = []
    for q in range(2):
        for n in range(BANDS):
            t, s = divmod(BRANCHES * n, LANES)
            halves = []
            for c in range(2):
                at = slice((2 * q + c) * BANDS, (2 * q + c + 1) * BANDS)
                piece = field[t][at]
                if s + BRANCHES > LANES:
                    piece = jnp.where(lane >= s, piece, field[t + 1][at])
                halves.append(turned(piece, SLOT * c - s))
            both = jnp.where(lane < SLOT, halves[0], halves[1])
            for g in range(BANDS // 8):
                top = 8 * (g * BANDS + n)
                spread[q, top : top + 8, :] = both[8 * g : 8 * (g + 1)]
        done = jnp.dot(
            spread[q].astype(jnp.bfloat16), e_ref[q], preferred_element_type=jnp.float32
        )
        modes_done.append(done.astype(jnp.bfloat16))

    block = u_ref.shape[1]
    for g in range(BANDS * BANDS // block):
        at = slice(g * block, (g + 1) * block)
        plain = jnp.concatenate([modes_done[0][at, :LANES], modes_done[1][at, :LANES]], 1)
        turned_by_i = jnp.concatenate([modes_done[0][at, LANES:], modes_done[1][at, LANES:]], 1)
        done = jnp.dot(u_ref[0], plain, preferred_element_type=jnp.float32) + jnp.dot(
            u_ref[1], turned_by_i, preferred_element_type=jnp.float32
        )
        for q in range(2):
            mixed[q, at, :] = done[:, q * LANES : (q + 1) * LANES]

    sends = []
    for q in range(2):
        for c in range(2):
            out = None
            for j in range(BANDS):
                t, s = divmod(BRANCHES * j, LANES)
                tops = [8 * (g * BANDS + j) for g in range(BANDS // 8)]
                piece = jnp.concatenate([mixed[q, top : top + 8, :] for top in tops], 0)
                piece = turned(piece, s - SLOT * c)
                out = piece if out is None else jnp.where(lane >= s, piece, out)
                if s + BRANCHES >= LANES:
                    ready[q, c, :, t * LANES : (t + 1) * LANES] = out
                    out = piece if s + BRANCHES > LANES else None
            sends.append(pltpu.make_async_copy(ready.at[q, c], o_ref.at[q, c], sems.at[q, c]))
            sends[-1].start()
    for send in sends:
        send.wait()


def room(mib):
    return pltpu.CompilerParams(vmem_limit_bytes=mib * 2**20)


def vmem(shape, dtype):
    return jax.ShapeDtypeStruct(shape, dtype)


def local(wannier_g, rp_coords, q_coords, k_index, k_vectors, kq_vectors, modes):
    groups = lax.axis_size("rp")
    columns = lax.axis_size("pb")
    devices = groups * columns
    per_device = q_coords.shape[1]
    span = wannier_g.shape[1]
    rows = 2 * span
    cut = rows * EXTRA // LANES
    chunk = rows + cut + 8

    sent = jnp.broadcast_to(q_coords[None], (columns, 3, per_device))
    near = lax.all_to_all(sent, "pb", split_axis=0, concat_axis=0, tiled=True)
    near = near.transpose(1, 0, 2).reshape(3, columns * per_device)
    near = jnp.pad(near.astype(jnp.bfloat16), ((0, 5), (0, LANES - columns * per_device)))
    packed = pl.pallas_call(
        pack_kernel,
        out_shape=vmem((groups, chunk, LANES), jnp.bfloat16),
        in_specs=[pl.BlockSpec(memory_space=pltpu.HBM)],
        out_specs=pl.BlockSpec(memory_space=pl.ANY),
        scratch_shapes=[
            pltpu.VMEM((rows, LANES), jnp.bfloat16),
            pltpu.VMEM((groups, cut, LANES), jnp.bfloat16),
            pltpu.SemaphoreType.DMA((groups + 2,)),
        ],
        compiler_params=room(8),
        name="pack",
    )(pltpu.with_memory_space_constraint(wannier_g.reshape(rows, wannier_g.shape[3]), pltpu.HBM))
    packed = packed.at[:, rows + cut :, :].set(jnp.broadcast_to(near, (groups, 8, LANES)))
    turns_of = jnp.pad(rp_coords.astype(jnp.float32) / NK, ((0, 5), (0, 0)))
    turns_of = turns_of.astype(jnp.bfloat16)
    select = (jnp.arange(k_vectors.shape[0]) == k_index[0]).astype(jnp.bfloat16)
    unit = jnp.einsum("k,kcnj->cnj", select, k_vectors, preferred_element_type=jnp.float32)
    span8 = jnp.arange(8 * BANDS)
    wide = (span8[:, None] // 8 == jnp.arange(BANDS)).astype(jnp.bfloat16)
    u_table = jnp.einsum(
        "pj,cnj->cpn", wide, unit.astype(jnp.bfloat16), preferred_element_type=jnp.float32
    ).astype(jnp.bfloat16)
    u_table = jnp.einsum("cpn,kn->cpk", u_table, wide, preferred_element_type=jnp.float32)
    u_table = jnp.where(span8[:, None] % 8 == span8 % 8, u_table, 0.0).astype(jnp.bfloat16)
    v_real, v_imag = kq_vectors[:, 0], kq_vectors[:, 1]
    v_block = jnp.stack([jnp.stack([v_real, -v_imag], 2), jnp.stack([v_imag, v_real], 2)], 1)
    twice = jnp.repeat(jnp.eye(2 * BANDS, dtype=jnp.bfloat16), per_device, 1)
    v_table = jnp.einsum(
        "qcmdi,cmk->qdik",
        v_block,
        twice.reshape(2, BANDS, 2 * BANDS * per_device),
        preferred_element_type=jnp.float32,
    ).reshape(per_device, 2 * BANDS, 2 * BANDS * per_device)
    own = jnp.arange(2 * BANDS * per_device) % per_device == jnp.arange(per_device)[:, None]
    v_table = jnp.where(own[:, None, :], v_table, 0.0).astype(jnp.bfloat16)
    v_table = v_table.reshape(per_device * 2 * BANDS, 2 * BANDS * per_device)
    rest = SLOT - BRANCHES
    e_pad = jnp.pad(modes, ((0, 0), (0, 0), (0, rest), (0, rest)))
    e_real, e_imag = e_pad[:, 0], e_pad[:, 1]
    e_table = jnp.concatenate(
        [
            jnp.concatenate([e_real, e_imag, -e_imag, e_real], 2),
            jnp.concatenate([-e_imag, e_real, -e_real, -e_imag], 2),
        ],
        1,
    )
    moved = lax.all_to_all(packed, "rp", split_axis=0, concat_axis=0, tiled=True)

    vectors = rp_coords.shape[1]
    total = devices * per_device
    fourier = pl.pallas_call(
        fourier_kernel,
        out_shape=vmem((devices, 3, per_device, LANES), jnp.bfloat16),
        scratch_shapes=[
            pltpu.VMEM((total, 2 * vectors), jnp.bfloat16),
            pltpu.VMEM((2 * vectors, 3 * LANES), jnp.bfloat16),
        ],
        compiler_params=room(16),
        name="fourier",
    )(moved, turns_of)
    fourier, u_table, v_table, e_table = lax.optimization_barrier(
        (fourier, u_table, v_table, e_table)
    )
    owned = lax.all_to_all(fourier, AXES, split_axis=0, concat_axis=0, tiled=True)
    owned = owned.reshape(groups, columns, 3, per_device, LANES)

    return pl.pallas_call(
        rotate_kernel,
        out_shape=vmem((per_device, 2, BANDS, BANDS * BRANCHES), jnp.float32),
        scratch_shapes=[
            pltpu.VMEM((per_device, BANDS * BANDS, LANES), jnp.float32),
            pltpu.VMEM((per_device, BANDS * BANDS, LANES), jnp.float32),
            pltpu.VMEM((per_device, 2, BANDS, BANDS * BRANCHES), jnp.float32),
            pltpu.SemaphoreType.DMA((per_device, 2)),
        ],
        out_specs=pl.BlockSpec(memory_space=pl.ANY),
        compiler_params=room(16),
        name="rotate",
    )(owned, v_table, e_table, u_table)


def solution(mesh):
    return jax.shard_map(
        local,
        mesh=mesh,
        in_specs=(
            P(None, "rp", "pb", None),
            P(),
            P(None, AXES),
            P(),
            P(),
            P(AXES, None, None, None),
            P(AXES, None, None, None),
        ),
        out_specs=P(AXES, None, None, None),
        check_vma=False,
    )
```

time: 70.5 us -> 83.9 us (1.19)
  Pallas kernels: 7.13 us -> 22.3 us
  waiting for transfers between devices: 14.8 us -> 8.16 us
  blocking collectives: 24.9 us -> 29.8 us
    pallas_call x1, Pallas kernels: 1.04 us -> 17.1 us  [local(): pl.pallas_call(pack_kernel, out_shape=vmem((groups, chunk, LANES), jnp.bf...]
    all_to_all x1, waiting for transfers between devices: 6.69 us -> 0.01 us  [local(): near = lax.all_to_all(sent, 'pb', split_axis=0, concat_axis=0, tiled=True)]
    all_to_all x1, blocking collectives: 24.9 us -> 29.8 us  [local(): lax.all_to_all(fourier, AXES, split_axis=0, concat_axis=0, tiled=True)]
    pallas_call x1, Pallas kernels: 3.31 us -> 2.43 us  [local(): pl.pallas_call(rotate_kernel, out_shape=vmem((per_device, 2, BANDS, BANDS...]
  transfers between devices with their start and end apart: 2 -> 2, of which waited for: 2 -> 1; matrix products, arithmetic and copies ran while one was open for 3% -> 2% of each run, Pallas kernels for 1% -> 20%
where the time goes in v4:
time: 83.9 us; the launch traced here: 83.4 us
  blocking collectives  29.8 us (36%)
  Pallas kernels  22.3 us (27%)
  starting transfers between devices  17.3 us (21%)
  waiting for transfers between devices  8.16 us (10%)
  local copies, waits for them, and re-layouts  3.84 us (5%)
  between operations  0.85 us (1%)
    all_to_all x1, blocking collectives, local(): lax.all_to_all(fourier, AXES, split_axis=0, concat_axis=0, tiled=True)  29.8 us
    pallas_call x1, Pallas kernels, local(): pl.pallas_call(pack_kernel, out_shape=vmem((groups, chunk, LANES), jnp.bf...  17.1 us
    all_to_all x1, starting transfers between devices, local(): near = lax.all_to_all(sent, 'pb', split_axis=0, concat_axis=0, tiled=True)  12.9 us
    all_to_all x1, waiting for transfers between devices, local(): lax.all_to_all(packed, 'rp', split_axis=0, concat_axis=0, tiled=True)  8.16 us
    all_to_all x1, starting transfers between devices, local(): lax.all_to_all(packed, 'rp', split_axis=0, concat_axis=0, tiled=True)  4.47 us
    pallas_call x1, Pallas kernels, local(): pl.pallas_call(fourier_kernel, out_shape=vmem((devices, 3, per_device, LA...  2.78 us
    pallas_call x1, Pallas kernels, local(): pl.pallas_call(rotate_kernel, out_shape=vmem((per_device, 2, BANDS, BANDS...  2.43 us
  transfers between devices with their start and end apart: 2, of which 1 were waited for; matrix products, arithmetic and copies ran while one was open for 2% of the time, Pallas kernels for 20%

profile of v4, /device:TPU:1, one launch (start us, length us, event | category | flops | bytes accessed | tf_op | source)
XLA Modules:
  0.0 83.4 jit_solution(18350218060141635353)
XLA Ops:
  0.0 0.0 copy-start
  0.0 1.3 %broadcast_in_dim.20 = s32[32,3,2]{1,2,0:T(2,128)} broadcast(s32[3,2]{0,1:T(2,128)} %param.11), dimensions={1,2} | broadcast | bytes 792 | tf_op jit(solution)/shard_map/broadcast_in_dim | solution.py:205
  1.3 0.0 copy-start.2
  1.3 12.9 %all-to-all-start = ((s32[32,3,2]{1,2,0:T(2,128)}), s32[32,3,2]{1,2,0:T(2,128)S(1)}, u32[]{:S(2)}, u32[]{:S(2)}) async-start(s32[32,3,2]{1,2,0:T(2,128)} %broadcast_in_dim.20), calls=%async_computation | async-start | bytes 65536 | tf_op jit(solution)/shard_map/all_to_all | solution.py:206
  14.2 0.0 copy-done.2
  14.3 0.0 copy-start.1
  14.3 0.7 copy-done.1
  15.0 0.0 copy-start.3
  15.1 0.7 copy-done.3
  15.8 17.1 %pack.1 = bf16[8,296,128]{2,1,0:T(8,128)(2,1)} custom-call(bf16[256,1152]{1,0:T(8,128)(2,1)} %bitcast.62), custom_call_target="tpu_custom_call" | custom-call | tf_op jit(solution)/shard_map/pack/pallas_call | solution.py:209
  32.9 0.0 all-to-all-done
  32.9 0.1 copy.26
  33.0 0.6 broadcast_dynamic-update-slice_fusion
  33.7 4.5 %all-to-all-start.1 = ((bf16[8,296,128]{2,1,0:T(8,128)(2,1)}), bf16[8,296,128]{2,1,0:T(8,128)(2,1)S(1)}, u32[]{:S(2)}, u32[]{:S(2)}) async-start(bf16[8,296,128]{2,1,0:T(8,128)(2,1)} %broadcast_dynamic-update-slice_fusion), calls=%async_computation.1 | async-start | bytes 1212416 | tf_op jit(solution)/shard_map/all_to_all | solution.py:256
  38.1 0.1 copy.19
  38.2 0.1 dot_general.20
  38.3 0.1 reshape_reshape.3
  38.4 0.1 copy.20
  39.2 0.1 maximum_maximum_fusion.e_ref
  39.3 0.1 broadcast_compare_fusion
  39.4 0.2 fusion.2
  39.6 0.0 copy-done
  39.6 0.2 fusion.4
  39.8 0.4 fusion.u_ref
  40.2 8.2 %all-to-all-done.1.x_ref = bf16[8,296,128]{2,1,0:T(8,128)(2,1)S(1)} async-done(((bf16[8,296,128]{2,1,0:T(8,128)(2,1)}), bf16[8,296,128]{2,1,0:T(8,128)(2,1)S(1)}, u32[]{:S(2)}, u32[]{:S(2)}) %all-to-all-start.1) | async-done | bytes 606240 | tf_op jit(solution)/shard_map/all_to_all | solution.py:256
  48.4 2.8 %fourier.1 = bf16[256,3,2,128]{3,2,1,0:T(2,128)(2,1)S(1)} custom-call(bf16[8,296,128]{2,1,0:T(8,128)(2,1)S(1)} %all-to-all-done.1.x_ref, bf16[8,1024]{1,0:T(8,128)(2,1)S(1)} %pad.16.r_ref), custom_call_target="tpu_custom_call" | custom-call | tf_op jit(solution)/shard_map/fourier/pallas_call | solution.py:260
  51.2 29.8 %all_to_all.15 = bf16[256,3,2,128]{3,2,1,0:T(2,128)(2,1)S(1)} all-to-all(bf16[256,3,2,128]{3,2,1,0:T(2,128)(2,1)S(1)} %fourier.1), channel_id=1, replica_groups=mesh['rp'=8,'pb'=32] {'rp','pb'}, dimensions={0} | all-to-all | bytes 786432 | tf_op jit(solution)/shard_map/all_to_all | solution.py:273
  81.0 2.4 %rotate.1 = f32[2,2,32,1152]{3,2,1,0:T(8,128)} custom-call(bf16[8,32,3,2,128]{4,3,2,1,0:T(2,128)(2,1)S(1)} %bitcast.60, bf16[128,128]{1,0:T(8,128)(2,1)S(1)} %bitcast.61, bf16[2,128,256]{2,1,0:T(8,128)(2,1)S(1)} %maximum_maximum_fusion.e_ref, bf16[2,256,256]{2,1,0:T(8,128)(2,1)S(1)} %fusion.u_ref), custom_call_target="tpu_custom_call" | custom-call | tf_op jit(solution)/shard_map/rotate/pallas_call | solution.py:276
  (17 shorter events, 0.2 us)
Async XLA Ops:
  0.0 39.6 %copy-start = (bf16[8,2,32,32]{3,2,1,0:T(8,128)(2,1)S(1)}, bf16[8,2,32,32]{3,2,1,0:T(8,128)(2,1)}, u32[]{:S(2)}) copy-start(bf16[8,2,32,32]{3,2,1,0:T(8,128)(2,1)} %param.13) | copy-start | bytes 98308
  1.3 12.9 %copy-start.2 = (bf16[2,2,36,36]{3,1,2,0:T(2,128)(2,1)S(1)}, bf16[2,2,36,36]{3,1,2,0:T(2,128)(2,1)}, u32[]{:S(2)}) copy-start(bf16[2,2,36,36]{3,1,2,0:T(2,128)(2,1)} %param.15) | copy-start | bytes 31108
  1.3 31.6 %all-to-all-start = ((s32[32,3,2]{1,2,0:T(2,128)}), s32[32,3,2]{1,2,0:T(2,128)S(1)}, u32[]{:S(2)}, u32[]{:S(2)}) async-start(s32[32,3,2]{1,2,0:T(2,128)} %broadcast_in_dim.20), calls=%async_computation | async-start | bytes 65536 | tf_op jit(solution)/shard_map/all_to_all | solution.py:206
  14.3 0.8 copy-start.1
  15.0 0.7 copy-start.3
  33.7 14.7 %all-to-all-start.1 = ((bf16[8,296,128]{2,1,0:T(8,128)(2,1)}), bf16[8,296,128]{2,1,0:T(8,128)(2,1)S(1)}, u32[]{:S(2)}, u32[]{:S(2)}) async-start(bf16[8,296,128]{2,1,0:T(8,128)(2,1)} %broadcast_dynamic-update-slice_fusion), calls=%async_computation.1 | async-start | bytes 1212416 | tf_op jit(solution)/shard_map/all_to_all | solution.py:256

commit v5 on v4

--- a/solution.py
+++ b/solution.py
@@ -20,9 +20,10 @@
 
 def sine_series():
     points = np.arange(1, 5) / NK
-    powers = np.stack([points ** (2 * k) for k in range(4)], 1)
-    values = np.sin(2 * math.pi * points) / points
-    return [float(c) for c in np.linalg.solve(powers, values)]
+    slack = np.array([1e3, 5e2, 2e4, 5e2])
+    powers = np.stack([points ** (2 * k + 1) for k in range(3)], 1)
+    values = np.sin(2 * math.pi * points)
+    return [float(c) for c in np.linalg.lstsq(powers * slack[:, None], values * slack, rcond=None)[0]]
 
 
 SERIES = sine_series()
@@ -37,22 +38,15 @@
     return pltpu.roll(x, shift, 1) if shift else x
 
 
-def pack_kernel(w_ref, o_ref, tail_ref, cut_ref, sems):
-    groups, cut, _ = cut_ref.shape
+def pack_kernel(w_ref, o_ref):
+    groups = o_ref.shape[0]
     rows = w_ref.shape[0]
+    cut = rows * EXTRA // LANES
     pieces = rows // cut
-    fetch = pltpu.make_async_copy(w_ref.at[:, groups * LANES :], tail_ref, sems.at[groups])
-    fetch.start()
-    moves = [
-        pltpu.make_async_copy(
-            w_ref.at[:, a * LANES : (a + 1) * LANES], o_ref.at[a, :rows, :], sems.at[a]
-        )
-        for a in range(groups)
-    ]
-    for move in moves:
-        move.start()
-    fetch.wait()
-    tail = tail_ref[...].astype(jnp.float32)
+    for a in range(groups):
+        o_ref[a, :rows, :] = w_ref[:, a * LANES : (a + 1) * LANES]
+        o_ref[a, rows + cut :, :] = jnp.zeros((o_ref.shape[1] - rows - cut, LANES), o_ref.dtype)
+    tail = w_ref[:, groups * LANES :].astype(jnp.float32)
     lane = lane_of((cut, LANES))
     half = pieces // 2
     for a in range(groups):
@@ -61,19 +55,14 @@
             place = 2 * (j % half) + j // half
             piece = turned(tail[j * cut : (j + 1) * cut], EXTRA * (place - a))
             mixed = jnp.where(lane // EXTRA == place, piece, mixed)
-        cut_ref[a] = mixed.astype(o_ref.dtype)
-    last = pltpu.make_async_copy(cut_ref, o_ref.at[:, rows : rows + cut, :], sems.at[groups + 1])
-    last.start()
-    for move in moves:
-        move.wait()
-    last.wait()
+        o_ref[a, rows : rows + cut, :] = mixed.astype(o_ref.dtype)
 
 
 def wave(u):
     w = 0.25 - jnp.abs(u - jnp.round(u))
     s = w * w
-    value = SERIES[3]
-    for c in SERIES[2::-1]:
+    value = SERIES[2]
+    for c in SERIES[1::-1]:
         value = value * s + c
     return value * w
 
@@ -91,10 +80,12 @@
     for a in range(groups):
         coords = x_ref[a, rows + cut :, :].astype(jnp.float32)
         q_rows = coords.T[:per_group].astype(jnp.bfloat16)
-        turns = jnp.dot(q_rows, r_all, preferred_element_type=jnp.float32)
         at = slice(a * per_group, (a + 1) * per_group)
-        left[at, :vectors] = wave(turns).astype(jnp.bfloat16)
-        left[at, vectors:] = wave(turns - 0.25).astype(jnp.bfloat16)
+        for n in range(0, vectors, 2 * LANES):
+            end = n + 2 * LANES
+            turns = jnp.dot(q_rows, r_all[:, n:end], preferred_element_type=jnp.float32)
+            left[at, n:end] = wave(turns).astype(jnp.bfloat16)
+            left[at, vectors + n : vectors + end] = wave(turns - 0.25).astype(jnp.bfloat16)
     for a in range(groups):
         real = x_ref[a, :span, :]
         imag = x_ref[a, span:rows, :]
@@ -209,16 +200,9 @@
     packed = pl.pallas_call(
         pack_kernel,
         out_shape=vmem((groups, chunk, LANES), jnp.bfloat16),
-        in_specs=[pl.BlockSpec(memory_space=pltpu.HBM)],
-        out_specs=pl.BlockSpec(memory_space=pl.ANY),
-        scratch_shapes=[
-            pltpu.VMEM((rows, LANES), jnp.bfloat16),
-            pltpu.VMEM((groups, cut, LANES), jnp.bfloat16),
-            pltpu.SemaphoreType.DMA((groups + 2,)),
-        ],
         compiler_params=room(8),
         name="pack",
-    )(pltpu.with_memory_space_constraint(wannier_g.reshape(rows, wannier_g.shape[3]), pltpu.HBM))
+    )(wannier_g.reshape(rows, wannier_g.shape[3]))
     packed = packed.at[:, rows + cut :, :].set(jnp.broadcast_to(near, (groups, 8, LANES)))
     turns_of = jnp.pad(rp_coords.astype(jnp.float32) / NK, ((0, 5), (0, 0)))
     turns_of = turns_of.astype(jnp.bfloat16)

time: 83.9 us -> 69.4 us (0.83)
  Pallas kernels: 22.3 us -> 6 us
  waiting for transfers between devices: 8.16 us -> 13.5 us
  blocking collectives: 29.8 us -> 24.9 us
  other arithmetic: 0.33 us -> 1.77 us
    pallas_call x1, Pallas kernels: 17.1 us -> 1.04 us  [local(): pl.pallas_call(pack_kernel, out_shape=vmem((groups, chunk, LANES), jnp.bf...]
    all_to_all x1, waiting for transfers between devices: 0.01 us -> 5.55 us  [local(): near = lax.all_to_all(sent, 'pb', split_axis=0, concat_axis=0, tiled=True)]
    all_to_all x1, blocking collectives: 29.8 us -> 24.9 us  [local(): lax.all_to_all(fourier, AXES, split_axis=0, concat_axis=0, tiled=True)]
  transfers between devices with their start and end apart: 2 -> 2, of which waited for: 1 -> 2; matrix products, arithmetic and copies ran while one was open for 2% -> 6% of each run, Pallas kernels for 20% -> 2%
where the time goes in v5:
time: 69.4 us; the launch traced here: 68.9 us
  blocking collectives  24.9 us (36%)
  starting transfers between devices  17.2 us (25%)
  waiting for transfers between devices  13.5 us (19%)
  Pallas kernels  6 us (9%)
  local copies, waits for them, and re-layouts  3.99 us (6%)
  other arithmetic  1.77 us (3%)
  between operations  0.79 us (1%)
  matrix products  0.78 us (1%)
    all_to_all x1, blocking collectives, local(): lax.all_to_all(fourier, AXES, split_axis=0, concat_axis=0, tiled=True)  24.9 us
    all_to_all x1, starting transfers between devices, local(): near = lax.all_to_all(sent, 'pb', split_axis=0, concat_axis=0, tiled=True)  12.7 us
    all_to_all x1, waiting for transfers between devices, local(): lax.all_to_all(packed, 'rp', split_axis=0, concat_axis=0, tiled=True)  7.99 us
    all_to_all x1, waiting for transfers between devices, local(): near = lax.all_to_all(sent, 'pb', split_axis=0, concat_axis=0, tiled=True)  5.55 us
    all_to_all x1, starting transfers between devices, local(): lax.all_to_all(packed, 'rp', split_axis=0, concat_axis=0, tiled=True)  4.44 us
    pallas_call x1, Pallas kernels, local(): pl.pallas_call(fourier_kernel, out_shape=vmem((devices, 3, per_device, LA...  2.54 us
    pallas_call x1, Pallas kernels, local(): pl.pallas_call(rotate_kernel, out_shape=vmem((per_device, 2, BANDS, BANDS...  2.43 us
  transfers between devices with their start and end apart: 2, of which 2 were waited for; matrix products, arithmetic and copies ran while one was open for 6% of the time, Pallas kernels for 2%

profile of v5, /device:TPU:1, one launch (start us, length us, event | category | flops | bytes accessed | tf_op | source)
XLA Modules:
  0.0 68.9 jit_solution(13780423568019235969)
XLA Ops:
  0.0 0.0 copy-start
  0.0 0.0 copy-start.1
  0.0 1.4 %broadcast_in_dim.20 = s32[32,3,2]{1,2,0:T(2,128)} broadcast(s32[3,2]{0,1:T(2,128)} %param.11), dimensions={1,2} | broadcast | bytes 792 | tf_op jit(solution)/shard_map/broadcast_in_dim | solution.py:196
  1.4 12.7 %all-to-all-start = ((s32[32,3,2]{1,2,0:T(2,128)}), s32[32,3,2]{1,2,0:T(2,128)S(1)}, u32[]{:S(2)}, u32[]{:S(2)}) async-start(s32[32,3,2]{1,2,0:T(2,128)} %broadcast_in_dim.20), calls=%async_computation | async-start | bytes 65536 | tf_op jit(solution)/shard_map/all_to_all | solution.py:197
  14.1 0.8 %copy.21 = bf16[2,2,36,36]{3,2,0,1:T(8,128)(2,1)S(1)} copy(bf16[2,2,36,36]{3,1,2,0:T(2,128)(2,1)} %param.15) | data formatting | bytes 20736 | tf_op args[6]
  15.0 0.7 %slice_bitcast_fusion = (bf16[2,32,1,32]{3,1,0,2:T(8,128)(2,1)S(1)}, bf16[2,32,1,32]{3,1,0,2:T(8,128)(2,1)S(1)}) fusion(bf16[2,2,32,32]{3,2,1,0:T(8,128)(2,1)} %param.14), kind=kLoop, calls=%fused_computation.23 | loop fusion | bytes 16384 | tf_op jit(solution)/shard_map/squeeze | solution.py:218
  15.7 0.7 %fusion.22 = bf16[2,32,1,32]{3,1,0,2:T(8,128)(2,1)S(1)} fusion(bf16[2,2,32,32]{3,2,1,0:T(8,128)(2,1)} %param.14), kind=kLoop, calls=%fused_computation.41 | loop fusion | flops 2048 | bytes 8192 | tf_op jit(solution)/shard_map/neg | solution.py:219
  16.5 0.7 %multiply_convert_fusion = bf16[3,1024]{1,0:T(4,128)(2,1)S(1)} fusion(s32[3,1024]{1,0:T(4,128)} %param.10), kind=kLoop, calls=%fused_computation.27 | loop fusion | flops 9216 | bytes 18432 | tf_op jit(solution)/shard_map/convert
  17.2 0.0 copy-done.1
  17.2 1.0 %pack.1 = bf16[8,296,128]{2,1,0:T(8,128)(2,1)} custom-call(bf16[256,1152]{1,0:T(8,128)(2,1)S(1)} %bitcast.61), custom_call_target="tpu_custom_call" | custom-call | tf_op jit(solution)/shard_map/pack/pallas_call | solution.py:200
  18.3 5.6 %all-to-all-done = s32[32,3,2]{1,2,0:T(2,128)S(1)} async-done(((s32[32,3,2]{1,2,0:T(2,128)}), s32[32,3,2]{1,2,0:T(2,128)S(1)}, u32[]{:S(2)}, u32[]{:S(2)}) %all-to-all-start) | async-done | bytes 800 | tf_op jit(solution)/shard_map/all_to_all | solution.py:197
  23.9 0.1 copy.26
  23.9 0.6 broadcast_dynamic-update-slice_fusion
  24.6 4.4 %all-to-all-start.1 = ((bf16[8,296,128]{2,1,0:T(8,128)(2,1)}), bf16[8,296,128]{2,1,0:T(8,128)(2,1)S(1)}, u32[]{:S(2)}, u32[]{:S(2)}) async-start(bf16[8,296,128]{2,1,0:T(8,128)(2,1)} %broadcast_dynamic-update-slice_fusion), calls=%async_computation.1 | async-start | bytes 1212416 | tf_op jit(solution)/shard_map/all_to_all | solution.py:240
  29.0 0.1 copy.19
  29.1 0.1 dot_general.20
  29.2 0.1 reshape_reshape.3
  29.3 0.1 copy.20
  30.1 0.1 maximum_maximum_fusion.e_ref
  30.2 0.1 broadcast_compare_fusion
  30.3 0.2 fusion.2
  30.5 0.0 copy-done
  30.5 0.2 fusion.4
  30.7 0.4 fusion.u_ref
  31.1 8.0 %all-to-all-done.1.x_ref = bf16[8,296,128]{2,1,0:T(8,128)(2,1)S(1)} async-done(((bf16[8,296,128]{2,1,0:T(8,128)(2,1)}), bf16[8,296,128]{2,1,0:T(8,128)(2,1)S(1)}, u32[]{:S(2)}, u32[]{:S(2)}) %all-to-all-start.1) | async-done | bytes 606240 | tf_op jit(solution)/shard_map/all_to_all | solution.py:240
  39.1 2.5 %fourier.1 = bf16[256,3,2,128]{3,2,1,0:T(2,128)(2,1)S(1)} custom-call(bf16[8,296,128]{2,1,0:T(8,128)(2,1)S(1)} %all-to-all-done.1.x_ref, bf16[8,1024]{1,0:T(8,128)(2,1)S(1)} %pad.16.r_ref), custom_call_target="tpu_custom_call" | custom-call | tf_op jit(solution)/shard_map/fourier/pallas_call | solution.py:244
  41.6 24.9 %all_to_all.15 = bf16[256,3,2,128]{3,2,1,0:T(2,128)(2,1)S(1)} all-to-all(bf16[256,3,2,128]{3,2,1,0:T(2,128)(2,1)S(1)} %fourier.1), channel_id=1, replica_groups=mesh['rp'=8,'pb'=32] {'rp','pb'}, dimensions={0} | all-to-all | bytes 786432 | tf_op jit(solution)/shard_map/all_to_all | solution.py:257
  66.5 2.4 %rotate.1 = f32[2,2,32,1152]{3,2,1,0:T(8,128)} custom-call(bf16[8,32,3,2,128]{4,3,2,1,0:T(2,128)(2,1)S(1)} %bitcast.60, bf16[128,128]{1,0:T(8,128)(2,1)S(1)} %bitcast.62, bf16[2,128,256]{2,1,0:T(8,128)(2,1)S(1)} %maximum_maximum_fusion.e_ref, bf16[2,256,256]{2,1,0:T(8,128)(2,1)S(1)} %fusion.u_ref), custom_call_target="tpu_custom_call" | custom-call | tf_op jit(solution)/shard_map/rotate/pallas_call | solution.py:260
  (13 shorter events, 0.2 us)
Async XLA Ops:
  0.0 30.5 %copy-start = (bf16[8,2,32,32]{3,2,1,0:T(8,128)(2,1)S(1)}, bf16[8,2,32,32]{3,2,1,0:T(8,128)(2,1)}, u32[]{:S(2)}) copy-start(bf16[8,2,32,32]{3,2,1,0:T(8,128)(2,1)} %param.13) | copy-start | bytes 98308
  0.0 17.2 %copy-start.1 = (bf16[2,128,1,1152]{3,1,2,0:T(8,128)(2,1)S(1)}, bf16[2,128,1,1152]{3,1,2,0:T(8,128)(2,1)}, u32[]{:S(2)}) copy-start(bf16[2,128,1,1152]{3,1,2,0:T(8,128)(2,1)} %param.9) | copy-start | bytes 1769476
  1.4 22.5 %all-to-all-start = ((s32[32,3,2]{1,2,0:T(2,128)}), s32[32,3,2]{1,2,0:T(2,128)S(1)}, u32[]{:S(2)}, u32[]{:S(2)}) async-start(s32[32,3,2]{1,2,0:T(2,128)} %broadcast_in_dim.20), calls=%async_computation | async-start | bytes 65536 | tf_op jit(solution)/shard_map/all_to_all | solution.py:197
  24.6 14.5 %all-to-all-start.1 = ((bf16[8,296,128]{2,1,0:T(8,128)(2,1)}), bf16[8,296,128]{2,1,0:T(8,128)(2,1)S(1)}, u32[]{:S(2)}, u32[]{:S(2)}) async-start(bf16[8,296,128]{2,1,0:T(8,128)(2,1)} %broadcast_dynamic-update-slice_fusion), calls=%async_computation.1 | async-start | bytes 1212416 | tf_op jit(solution)/shard_map/all_to_all | solution.py:240

commit v6 on v5

--- a/solution.py
+++ b/solution.py
@@ -18,15 +18,15 @@
 AXES = ("rp", "pb")
 
 
-def sine_series():
-    points = np.arange(1, 5) / NK
-    slack = np.array([1e3, 5e2, 2e4, 5e2])
-    powers = np.stack([points ** (2 * k + 1) for k in range(3)], 1)
-    values = np.sin(2 * math.pi * points)
+def fitted(points, factor, values):
+    slack = np.where(np.abs(values - 0.924) < 0.01, 2e4, 1e3)
+    powers = np.stack([factor * points ** (2 * k) for k in range(3)], 1)
     return [float(c) for c in np.linalg.lstsq(powers * slack[:, None], values * slack, rcond=None)[0]]
 
 
-SERIES = sine_series()
+STEPS = np.arange(5) / NK
+ODD = fitted(STEPS[1:], STEPS[1:], np.sin(2 * math.pi * STEPS[1:]))
+EVEN = fitted(STEPS[:4], 1 / 16 - STEPS[:4] ** 2, np.cos(2 * math.pi * STEPS[:4]))
 
 
 def lane_of(shape):
@@ -58,13 +58,13 @@
         o_ref[a, rows : rows + cut, :] = mixed.astype(o_ref.dtype)
 
 
-def wave(u):
-    w = 0.25 - jnp.abs(u - jnp.round(u))
+def waves(u):
+    d = u - jnp.round(u)
+    w = 0.25 - jnp.abs(d)
     s = w * w
-    value = SERIES[2]
-    for c in SERIES[1::-1]:
-        value = value * s + c
-    return value * w
+    cosine = w * (ODD[0] + s * (ODD[1] + s * ODD[2]))
+    size = (1 / 16 - s) * (EVEN[0] + s * (EVEN[1] + s * EVEN[2]))
+    return cosine.astype(jnp.bfloat16), jnp.where(d < 0, -size, size).astype(jnp.bfloat16)
 
 
 def fourier_kernel(x_ref, r_ref, o_ref, left, right):
@@ -84,8 +84,7 @@
         for n in range(0, vectors, 2 * LANES):
             end = n + 2 * LANES
             turns = jnp.dot(q_rows, r_all[:, n:end], preferred_element_type=jnp.float32)
-            left[at, n:end] = wave(turns).astype(jnp.bfloat16)
-            left[at, vectors + n : vectors + end] = wave(turns - 0.25).astype(jnp.bfloat16)
+            left[at, n:end], left[at, vectors + n : vectors + end] = waves(turns)
     for a in range(groups):
         real = x_ref[a, :span, :]
         imag = x_ref[a, span:rows, :]
@@ -122,7 +121,11 @@
             part = jnp.where(lane // EXTRA == a, turned(tails[a], EXTRA * (a - c)), part)
         parts.append(part.astype(jnp.bfloat16))
     tiles.append(jnp.concatenate(parts, 0))
-    field = [jnp.dot(v_ref[...], t, preferred_element_type=jnp.float32) for t in tiles]
+    field = []
+    for t in range(0, len(tiles), 2):
+        pair = jnp.concatenate(tiles[t : t + 2], 1)
+        done = jnp.dot(v_ref[...], pair, preferred_element_type=jnp.float32)
+        field += [done[:, k : k + LANES] for k in range(0, pair.shape[1], LANES)]
 
     lane = lane_of((BANDS, LANES))
     modes_done = []

time: 69.4 us -> 69.3 us (level)
  no operation moved by 1% of the time
where the time goes in v6:
time: 69.3 us; the launch traced here: 68.8 us
  blocking collectives  24.9 us (36%)
  starting transfers between devices  17.2 us (25%)
  waiting for transfers between devices  13.5 us (19%)
  Pallas kernels  5.84 us (8%)
  local copies, waits for them, and re-layouts  3.99 us (6%)
  other arithmetic  1.77 us (3%)
  between operations  0.79 us (1%)
  matrix products  0.78 us (1%)
    all_to_all x1, blocking collectives, local(): lax.all_to_all(fourier, AXES, split_axis=0, concat_axis=0, tiled=True)  24.9 us
    all_to_all x1, starting transfers between devices, local(): near = lax.all_to_all(sent, 'pb', split_axis=0, concat_axis=0, tiled=True)  12.7 us
    all_to_all x1, waiting for transfers between devices, local(): lax.all_to_all(packed, 'rp', split_axis=0, concat_axis=0, tiled=True)  7.99 us
    all_to_all x1, waiting for transfers between devices, local(): near = lax.all_to_all(sent, 'pb', split_axis=0, concat_axis=0, tiled=True)  5.55 us
    all_to_all x1, starting transfers between devices, local(): lax.all_to_all(packed, 'rp', split_axis=0, concat_axis=0, tiled=True)  4.44 us
    pallas_call x1, Pallas kernels, local(): pl.pallas_call(rotate_kernel, out_shape=vmem((per_device, 2, BANDS, BANDS...  2.45 us
    pallas_call x1, Pallas kernels, local(): pl.pallas_call(fourier_kernel, out_shape=vmem((devices, 3, per_device, LA...  2.36 us
  transfers between devices with their start and end apart: 2, of which 2 were waited for; matrix products, arithmetic and copies ran while one was open for 6% of the time, Pallas kernels for 2%

profile of v6, /device:TPU:1, one launch (start us, length us, event | category | flops | bytes accessed | tf_op | source)
XLA Modules:
  0.0 68.8 jit_solution(12343780613238068019)
XLA Ops:
  0.0 0.0 copy-start
  0.0 0.0 copy-start.1
  0.0 1.4 %broadcast_in_dim.20 = s32[32,3,2]{1,2,0:T(2,128)} broadcast(s32[3,2]{0,1:T(2,128)} %param.11), dimensions={1,2} | broadcast | bytes 792 | tf_op jit(solution)/shard_map/broadcast_in_dim | solution.py:199
  1.4 12.7 %all-to-all-start = ((s32[32,3,2]{1,2,0:T(2,128)}), s32[32,3,2]{1,2,0:T(2,128)S(1)}, u32[]{:S(2)}, u32[]{:S(2)}) async-start(s32[32,3,2]{1,2,0:T(2,128)} %broadcast_in_dim.20), calls=%async_computation | async-start | bytes 65536 | tf_op jit(solution)/shard_map/all_to_all | solution.py:200
  14.1 0.8 %copy.21 = bf16[2,2,36,36]{3,2,0,1:T(8,128)(2,1)S(1)} copy(bf16[2,2,36,36]{3,1,2,0:T(2,128)(2,1)} %param.15) | data formatting | bytes 20736 | tf_op args[6]
  15.0 0.7 %slice_bitcast_fusion = (bf16[2,32,1,32]{3,1,0,2:T(8,128)(2,1)S(1)}, bf16[2,32,1,32]{3,1,0,2:T(8,128)(2,1)S(1)}) fusion(bf16[2,2,32,32]{3,2,1,0:T(8,128)(2,1)} %param.14), kind=kLoop, calls=%fused_computation.23 | loop fusion | bytes 16384 | tf_op jit(solution)/shard_map/squeeze | solution.py:221
  15.7 0.7 %fusion.22 = bf16[2,32,1,32]{3,1,0,2:T(8,128)(2,1)S(1)} fusion(bf16[2,2,32,32]{3,2,1,0:T(8,128)(2,1)} %param.14), kind=kLoop, calls=%fused_computation.41 | loop fusion | flops 2048 | bytes 8192 | tf_op jit(solution)/shard_map/neg | solution.py:222
  16.5 0.7 %multiply_convert_fusion = bf16[3,1024]{1,0:T(4,128)(2,1)S(1)} fusion(s32[3,1024]{1,0:T(4,128)} %param.10), kind=kLoop, calls=%fused_computation.27 | loop fusion | flops 9216 | bytes 18432 | tf_op jit(solution)/shard_map/convert
  17.2 0.0 copy-done.1
  17.2 1.0 %pack.1 = bf16[8,296,128]{2,1,0:T(8,128)(2,1)} custom-call(bf16[256,1152]{1,0:T(8,128)(2,1)S(1)} %bitcast.61), custom_call_target="tpu_custom_call" | custom-call | tf_op jit(solution)/shard_map/pack/pallas_call | solution.py:203
  18.3 5.6 %all-to-all-done = s32[32,3,2]{1,2,0:T(2,128)S(1)} async-done(((s32[32,3,2]{1,2,0:T(2,128)}), s32[32,3,2]{1,2,0:T(2,128)S(1)}, u32[]{:S(2)}, u32[]{:S(2)}) %all-to-all-start) | async-done | bytes 800 | tf_op jit(solution)/shard_map/all_to_all | solution.py:200
  23.9 0.1 copy.26
  23.9 0.6 broadcast_dynamic-update-slice_fusion
  24.6 4.4 %all-to-all-start.1 = ((bf16[8,296,128]{2,1,0:T(8,128)(2,1)}), bf16[8,296,128]{2,1,0:T(8,128)(2,1)S(1)}, u32[]{:S(2)}, u32[]{:S(2)}) async-start(bf16[8,296,128]{2,1,0:T(8,128)(2,1)} %broadcast_dynamic-update-slice_fusion), calls=%async_computation.1 | async-start | bytes 1212416 | tf_op jit(solution)/shard_map/all_to_all | solution.py:243
  29.0 0.1 copy.19
  29.1 0.1 dot_general.20
  29.2 0.1 reshape_reshape.3
  29.3 0.1 copy.20
  30.1 0.1 maximum_maximum_fusion.e_ref
  30.2 0.1 broadcast_compare_fusion
  30.3 0.2 fusion.2
  30.5 0.0 copy-done
  30.5 0.2 fusion.4
  30.7 0.4 fusion.u_ref
  31.1 8.0 %all-to-all-done.1.x_ref = bf16[8,296,128]{2,1,0:T(8,128)(2,1)S(1)} async-done(((bf16[8,296,128]{2,1,0:T(8,128)(2,1)}), bf16[8,296,128]{2,1,0:T(8,128)(2,1)S(1)}, u32[]{:S(2)}, u32[]{:S(2)}) %all-to-all-start.1) | async-done | bytes 606240 | tf_op jit(solution)/shard_map/all_to_all | solution.py:243
  39.1 2.4 %fourier.1 = bf16[256,3,2,128]{3,2,1,0:T(2,128)(2,1)S(1)} custom-call(bf16[8,296,128]{2,1,0:T(8,128)(2,1)S(1)} %all-to-all-done.1.x_ref, bf16[8,1024]{1,0:T(8,128)(2,1)S(1)} %pad.16.r_ref), custom_call_target="tpu_custom_call" | custom-call | tf_op jit(solution)/shard_map/fourier/pallas_call | solution.py:247
  41.5 24.9 %all_to_all.15 = bf16[256,3,2,128]{3,2,1,0:T(2,128)(2,1)S(1)} all-to-all(bf16[256,3,2,128]{3,2,1,0:T(2,128)(2,1)S(1)} %fourier.1), channel_id=1, replica_groups=mesh['rp'=8,'pb'=32] {'rp','pb'}, dimensions={0} | all-to-all | bytes 786432 | tf_op jit(solution)/shard_map/all_to_all | solution.py:260
  66.3 2.4 %rotate.1 = f32[2,2,32,1152]{3,2,1,0:T(8,128)} custom-call(bf16[8,32,3,2,128]{4,3,2,1,0:T(2,128)(2,1)S(1)} %bitcast.60, bf16[128,128]{1,0:T(8,128)(2,1)S(1)} %bitcast.62, bf16[2,128,256]{2,1,0:T(8,128)(2,1)S(1)} %maximum_maximum_fusion.e_ref, bf16[2,256,256]{2,1,0:T(8,128)(2,1)S(1)} %fusion.u_ref), custom_call_target="tpu_custom_call" | custom-call | tf_op jit(solution)/shard_map/rotate/pallas_call | solution.py:263
  (13 shorter events, 0.2 us)
Async XLA Ops:
  0.0 30.5 %copy-start = (bf16[8,2,32,32]{3,2,1,0:T(8,128)(2,1)S(1)}, bf16[8,2,32,32]{3,2,1,0:T(8,128)(2,1)}, u32[]{:S(2)}) copy-start(bf16[8,2,32,32]{3,2,1,0:T(8,128)(2,1)} %param.13) | copy-start | bytes 98308
  0.0 17.2 %copy-start.1 = (bf16[2,128,1,1152]{3,1,2,0:T(8,128)(2,1)S(1)}, bf16[2,128,1,1152]{3,1,2,0:T(8,128)(2,1)}, u32[]{:S(2)}) copy-start(bf16[2,128,1,1152]{3,1,2,0:T(8,128)(2,1)} %param.9) | copy-start | bytes 1769476
  1.4 22.5 %all-to-all-start = ((s32[32,3,2]{1,2,0:T(2,128)}), s32[32,3,2]{1,2,0:T(2,128)S(1)}, u32[]{:S(2)}, u32[]{:S(2)}) async-start(s32[32,3,2]{1,2,0:T(2,128)} %broadcast_in_dim.20), calls=%async_computation | async-start | bytes 65536 | tf_op jit(solution)/shard_map/all_to_all | solution.py:200
  24.6 14.5 %all-to-all-start.1 = ((bf16[8,296,128]{2,1,0:T(8,128)(2,1)}), bf16[8,296,128]{2,1,0:T(8,128)(2,1)S(1)}, u32[]{:S(2)}, u32[]{:S(2)}) async-start(bf16[8,296,128]{2,1,0:T(8,128)(2,1)} %broadcast_dynamic-update-slice_fusion), calls=%async_computation.1 | async-start | bytes 1212416 | tf_op jit(solution)/shard_map/all_to_all | solution.py:243

commit v7 on v6

--- a/solution.py
+++ b/solution.py
@@ -1,8 +1,5 @@
-import math
-
 import jax
 import jax.numpy as jnp
-import numpy as np
 from jax import lax
 from jax.experimental import pallas as pl
 from jax.experimental.pallas import tpu as pltpu
@@ -18,15 +15,7 @@
 AXES = ("rp", "pb")
 
 
-def fitted(points, factor, values):
-    slack = np.where(np.abs(values - 0.924) < 0.01, 2e4, 1e3)
-    powers = np.stack([factor * points ** (2 * k) for k in range(3)], 1)
-    return [float(c) for c in np.linalg.lstsq(powers * slack[:, None], values * slack, rcond=None)[0]]
-
-
-STEPS = np.arange(5) / NK
-ODD = fitted(STEPS[1:], STEPS[1:], np.sin(2 * math.pi * STEPS[1:]))
-EVEN = fitted(STEPS[:4], 1 / 16 - STEPS[:4] ** 2, np.cos(2 * math.pi * STEPS[:4]))
+ODD = (6.28125, -40.75, 68.5)
 
 
 def lane_of(shape):
@@ -58,13 +47,14 @@
         o_ref[a, rows : rows + cut, :] = mixed.astype(o_ref.dtype)
 
 
+def sine(w):
+    s = w * w
+    return w * (ODD[0] + s * (ODD[1] + s * ODD[2]))
+
+
 def waves(u):
-    d = u - jnp.round(u)
-    w = 0.25 - jnp.abs(d)
-    s = w * w
-    cosine = w * (ODD[0] + s * (ODD[1] + s * ODD[2]))
-    size = (1 / 16 - s) * (EVEN[0] + s * (EVEN[1] + s * EVEN[2]))
-    return cosine.astype(jnp.bfloat16), jnp.where(d < 0, -size, size).astype(jnp.bfloat16)
+    d = (u - jnp.round(u)).astype(jnp.bfloat16)
+    return sine(0.25 - jnp.abs(d)), sine(jnp.maximum(jnp.minimum(d, 0.5 - d), -0.5 - d))
 
 
 def fourier_kernel(x_ref, r_ref, o_ref, left, right):

time: 69.3 us -> 68.8 us (level)
  transfers between devices with their start and end apart: 2 -> 2, of which waited for: 2 -> 2; matrix products, arithmetic and copies ran while one was open for 6% -> 7% of each run, Pallas kernels for 2% -> 2%
where the time goes in v7:
time: 68.8 us; the launch traced here: 68.3 us
  blocking collectives  24.9 us (36%)
  starting transfers between devices  17.2 us (25%)
  waiting for transfers between devices  13.5 us (20%)
  Pallas kernels  5.39 us (8%)
  local copies, waits for them, and re-layouts  3.99 us (6%)
  other arithmetic  1.77 us (3%)
  between operations  0.79 us (1%)
  matrix products  0.78 us (1%)
    all_to_all x1, blocking collectives, local(): lax.all_to_all(fourier, AXES, split_axis=0, concat_axis=0, tiled=True)  24.9 us
    all_to_all x1, starting transfers between devices, local(): near = lax.all_to_all(sent, 'pb', split_axis=0, concat_axis=0, tiled=True)  12.7 us
    all_to_all x1, waiting for transfers between devices, local(): lax.all_to_all(packed, 'rp', split_axis=0, concat_axis=0, tiled=True)  7.99 us
    all_to_all x1, waiting for transfers between devices, local(): near = lax.all_to_all(sent, 'pb', split_axis=0, concat_axis=0, tiled=True)  5.55 us
    all_to_all x1, starting transfers between devices, local(): lax.all_to_all(packed, 'rp', split_axis=0, concat_axis=0, tiled=True)  4.44 us
    pallas_call x1, Pallas kernels, local(): pl.pallas_call(rotate_kernel, out_shape=vmem((per_device, 2, BANDS, BANDS...  2.44 us
    pallas_call x1, Pallas kernels, local(): pl.pallas_call(fourier_kernel, out_shape=vmem((devices, 3, per_device, LA...  1.91 us
  transfers between devices with their start and end apart: 2, of which 2 were waited for; matrix products, arithmetic and copies ran while one was open for 7% of the time, Pallas kernels for 2%

profile of v7, /device:TPU:1, one launch (start us, length us, event | category | flops | bytes accessed | tf_op | source)
XLA Modules:
  0.0 68.3 jit_solution(8367916148523169867)
XLA Ops:
  0.0 0.0 copy-start
  0.0 0.0 copy-start.1
  0.0 1.4 %broadcast_in_dim.20 = s32[32,3,2]{1,2,0:T(2,128)} broadcast(s32[3,2]{0,1:T(2,128)} %param.11), dimensions={1,2} | broadcast | bytes 792 | tf_op jit(solution)/shard_map/broadcast_in_dim | solution.py:189
  1.4 12.7 %all-to-all-start = ((s32[32,3,2]{1,2,0:T(2,128)}), s32[32,3,2]{1,2,0:T(2,128)S(1)}, u32[]{:S(2)}, u32[]{:S(2)}) async-start(s32[32,3,2]{1,2,0:T(2,128)} %broadcast_in_dim.20), calls=%async_computation | async-start | bytes 65536 | tf_op jit(solution)/shard_map/all_to_all | solution.py:190
  14.1 0.8 %copy.21 = bf16[2,2,36,36]{3,2,0,1:T(8,128)(2,1)S(1)} copy(bf16[2,2,36,36]{3,1,2,0:T(2,128)(2,1)} %param.15) | data formatting | bytes 20736 | tf_op args[6]
  15.0 0.7 %slice_bitcast_fusion = (bf16[2,32,1,32]{3,1,0,2:T(8,128)(2,1)S(1)}, bf16[2,32,1,32]{3,1,0,2:T(8,128)(2,1)S(1)}) fusion(bf16[2,2,32,32]{3,2,1,0:T(8,128)(2,1)} %param.14), kind=kLoop, calls=%fused_computation.23 | loop fusion | bytes 16384 | tf_op jit(solution)/shard_map/squeeze | solution.py:211
  15.7 0.7 %fusion.22 = bf16[2,32,1,32]{3,1,0,2:T(8,128)(2,1)S(1)} fusion(bf16[2,2,32,32]{3,2,1,0:T(8,128)(2,1)} %param.14), kind=kLoop, calls=%fused_computation.41 | loop fusion | flops 2048 | bytes 8192 | tf_op jit(solution)/shard_map/neg | solution.py:212
  16.5 0.7 %multiply_convert_fusion = bf16[3,1024]{1,0:T(4,128)(2,1)S(1)} fusion(s32[3,1024]{1,0:T(4,128)} %param.10), kind=kLoop, calls=%fused_computation.27 | loop fusion | flops 9216 | bytes 18432 | tf_op jit(solution)/shard_map/convert
  17.2 0.0 copy-done.1
  17.2 1.0 %pack.1 = bf16[8,296,128]{2,1,0:T(8,128)(2,1)} custom-call(bf16[256,1152]{1,0:T(8,128)(2,1)S(1)} %bitcast.61), custom_call_target="tpu_custom_call" | custom-call | tf_op jit(solution)/shard_map/pack/pallas_call | solution.py:193
  18.3 5.6 %all-to-all-done = s32[32,3,2]{1,2,0:T(2,128)S(1)} async-done(((s32[32,3,2]{1,2,0:T(2,128)}), s32[32,3,2]{1,2,0:T(2,128)S(1)}, u32[]{:S(2)}, u32[]{:S(2)}) %all-to-all-start) | async-done | bytes 800 | tf_op jit(solution)/shard_map/all_to_all | solution.py:190
  23.9 0.1 copy.26
  23.9 0.6 broadcast_dynamic-update-slice_fusion
  24.6 4.4 %all-to-all-start.1 = ((bf16[8,296,128]{2,1,0:T(8,128)(2,1)}), bf16[8,296,128]{2,1,0:T(8,128)(2,1)S(1)}, u32[]{:S(2)}, u32[]{:S(2)}) async-start(bf16[8,296,128]{2,1,0:T(8,128)(2,1)} %broadcast_dynamic-update-slice_fusion), calls=%async_computation.1 | async-start | bytes 1212416 | tf_op jit(solution)/shard_map/all_to_all | solution.py:233
  29.0 0.1 copy.19
  29.1 0.1 dot_general.20
  29.2 0.1 reshape_reshape.3
  29.3 0.1 copy.20
  30.1 0.1 maximum_maximum_fusion.e_ref
  30.2 0.1 broadcast_compare_fusion
  30.3 0.2 fusion.2
  30.5 0.0 copy-done
  30.5 0.2 fusion.4
  30.7 0.4 fusion.u_ref
  31.1 8.0 %all-to-all-done.1.x_ref = bf16[8,296,128]{2,1,0:T(8,128)(2,1)S(1)} async-done(((bf16[8,296,128]{2,1,0:T(8,128)(2,1)}), bf16[8,296,128]{2,1,0:T(8,128)(2,1)S(1)}, u32[]{:S(2)}, u32[]{:S(2)}) %all-to-all-start.1) | async-done | bytes 606240 | tf_op jit(solution)/shard_map/all_to_all | solution.py:233
  39.1 1.9 %fourier.1 = bf16[256,3,2,128]{3,2,1,0:T(2,128)(2,1)S(1)} custom-call(bf16[8,296,128]{2,1,0:T(8,128)(2,1)S(1)} %all-to-all-done.1.x_ref, bf16[8,1024]{1,0:T(8,128)(2,1)S(1)} %pad.16.r_ref), custom_call_target="tpu_custom_call" | custom-call | tf_op jit(solution)/shard_map/fourier/pallas_call | solution.py:237
  41.0 24.9 %all_to_all.15 = bf16[256,3,2,128]{3,2,1,0:T(2,128)(2,1)S(1)} all-to-all(bf16[256,3,2,128]{3,2,1,0:T(2,128)(2,1)S(1)} %fourier.1), channel_id=1, replica_groups=mesh['rp'=8,'pb'=32] {'rp','pb'}, dimensions={0} | all-to-all | bytes 786432 | tf_op jit(solution)/shard_map/all_to_all | solution.py:250
  65.9 2.4 %rotate.1 = f32[2,2,32,1152]{3,2,1,0:T(8,128)} custom-call(bf16[8,32,3,2,128]{4,3,2,1,0:T(2,128)(2,1)S(1)} %bitcast.60, bf16[128,128]{1,0:T(8,128)(2,1)S(1)} %bitcast.62, bf16[2,128,256]{2,1,0:T(8,128)(2,1)S(1)} %maximum_maximum_fusion.e_ref, bf16[2,256,256]{2,1,0:T(8,128)(2,1)S(1)} %fusion.u_ref), custom_call_target="tpu_custom_call" | custom-call | tf_op jit(solution)/shard_map/rotate/pallas_call | solution.py:253
  (13 shorter events, 0.2 us)
Async XLA Ops:
  0.0 30.5 %copy-start = (bf16[8,2,32,32]{3,2,1,0:T(8,128)(2,1)S(1)}, bf16[8,2,32,32]{3,2,1,0:T(8,128)(2,1)}, u32[]{:S(2)}) copy-start(bf16[8,2,32,32]{3,2,1,0:T(8,128)(2,1)} %param.13) | copy-start | bytes 98308
  0.0 17.2 %copy-start.1 = (bf16[2,128,1,1152]{3,1,2,0:T(8,128)(2,1)S(1)}, bf16[2,128,1,1152]{3,1,2,0:T(8,128)(2,1)}, u32[]{:S(2)}) copy-start(bf16[2,128,1,1152]{3,1,2,0:T(8,128)(2,1)} %param.9) | copy-start | bytes 1769476
  1.4 22.5 %all-to-all-start = ((s32[32,3,2]{1,2,0:T(2,128)}), s32[32,3,2]{1,2,0:T(2,128)S(1)}, u32[]{:S(2)}, u32[]{:S(2)}) async-start(s32[32,3,2]{1,2,0:T(2,128)} %broadcast_in_dim.20), calls=%async_computation | async-start | bytes 65536 | tf_op jit(solution)/shard_map/all_to_all | solution.py:190
  24.6 14.5 %all-to-all-start.1 = ((bf16[8,296,128]{2,1,0:T(8,128)(2,1)}), bf16[8,296,128]{2,1,0:T(8,128)(2,1)S(1)}, u32[]{:S(2)}, u32[]{:S(2)}) async-start(bf16[8,296,128]{2,1,0:T(8,128)(2,1)} %broadcast_dynamic-update-slice_fusion), calls=%async_computation.1 | async-start | bytes 1212416 | tf_op jit(solution)/shard_map/all_to_all | solution.py:233

commit v8 on v7

--- a/solution.py
+++ b/solution.py
@@ -71,8 +71,8 @@
         coords = x_ref[a, rows + cut :, :].astype(jnp.float32)
         q_rows = coords.T[:per_group].astype(jnp.bfloat16)
         at = slice(a * per_group, (a + 1) * per_group)
-        for n in range(0, vectors, 2 * LANES):
-            end = n + 2 * LANES
+        for n in range(0, vectors, 4 * LANES):
+            end = n + 4 * LANES
             turns = jnp.dot(q_rows, r_all[:, n:end], preferred_element_type=jnp.float32)
             left[at, n:end], left[at, vectors + n : vectors + end] = waves(turns)
     for a in range(groups):
@@ -96,7 +96,7 @@
         o_ref[:, k] = part.reshape(o_ref.shape[0], 2, LANES)
 
 
-def rotate_kernel(x_ref, v_ref, e_ref, u_ref, o_ref, spread, mixed, ready, sems):
+def rotate_kernel(x_ref, v_ref, e_ref, u_ref, o_ref, ready, sems):
     groups = x_ref.shape[0]
     pairs = 2 * BANDS
     lane = lane_of((pairs, LANES))
@@ -117,53 +117,46 @@
         done = jnp.dot(v_ref[...], pair, preferred_element_type=jnp.float32)
         field += [done[:, k : k + LANES] for k in range(0, pair.shape[1], LANES)]
 
-    lane = lane_of((BANDS, LANES))
-    modes_done = []
-    for q in range(2):
-        for n in range(BANDS):
-            t, s = divmod(BRANCHES * n, LANES)
-            halves = []
+    lane = lane_of((8, LANES))
+    sends = []
+    for g in range(BANDS // 8):
+        plain, by_i = [], []
+        for q in range(2):
+            rows = []
+            for n in range(BANDS):
+                t, s = divmod(BRANCHES * n, LANES)
+                halves = []
+                for c in range(2):
+                    top = (2 * q + c) * BANDS + 8 * g
+                    piece = field[t][top : top + 8]
+                    if s + BRANCHES > LANES:
+                        piece = jnp.where(lane >= s, piece, field[t + 1][top : top + 8])
+                    halves.append(turned(piece, SLOT * c - s))
+                rows.append(jnp.where(lane < SLOT, halves[0], halves[1]))
+            gathered = jnp.concatenate(rows, 0).astype(jnp.bfloat16)
+            done = jnp.dot(gathered, e_ref[q], preferred_element_type=jnp.float32)
+            done = done.astype(jnp.bfloat16)
+            plain.append(done[:, :LANES])
+            by_i.append(done[:, LANES:])
+        mixed = jnp.dot(
+            u_ref[0], jnp.concatenate(plain, 1), preferred_element_type=jnp.float32
+        ) + jnp.dot(u_ref[1], jnp.concatenate(by_i, 1), preferred_element_type=jnp.float32)
+        here = slice(8 * g, 8 * (g + 1))
+        for q in range(2):
             for c in range(2):
-                at = slice((2 * q + c) * BANDS, (2 * q + c + 1) * BANDS)
-                piece = field[t][at]
-                if s + BRANCHES > LANES:
-                    piece = jnp.where(lane >= s, piece, field[t + 1][at])
-                halves.append(turned(piece, SLOT * c - s))
-            both = jnp.where(lane < SLOT, halves[0], halves[1])
-            for g in range(BANDS // 8):
-                top = 8 * (g * BANDS + n)
-                spread[q, top : top + 8, :] = both[8 * g : 8 * (g + 1)]
-        done = jnp.dot(
-            spread[q].astype(jnp.bfloat16), e_ref[q], preferred_element_type=jnp.float32
+                out = None
+                for j in range(BANDS):
+                    t, s = divmod(BRANCHES * j, LANES)
+                    piece = mixed[8 * j : 8 * (j + 1), q * LANES : (q + 1) * LANES]
+                    piece = turned(piece, s - SLOT * c)
+                    out = piece if out is None else jnp.where(lane >= s, piece, out)
+                    if s + BRANCHES >= LANES:
+                        ready[q, c, here, t * LANES : (t + 1) * LANES] = out
+                        out = piece if s + BRANCHES > LANES else None
+        sends.append(
+            pltpu.make_async_copy(ready.at[:, :, here], o_ref.at[:, :, here], sems.at[g])
         )
-        modes_done.append(done.astype(jnp.bfloat16))
-
-    block = u_ref.shape[1]
-    for g in range(BANDS * BANDS // block):
-        at = slice(g * block, (g + 1) * block)
-        plain = jnp.concatenate([modes_done[0][at, :LANES], modes_done[1][at, :LANES]], 1)
-        turned_by_i = jnp.concatenate([modes_done[0][at, LANES:], modes_done[1][at, LANES:]], 1)
-        done = jnp.dot(u_ref[0], plain, preferred_element_type=jnp.float32) + jnp.dot(
-            u_ref[1], turned_by_i, preferred_element_type=jnp.float32
-        )
-        for q in range(2):
-            mixed[q, at, :] = done[:, q * LANES : (q + 1) * LANES]
-
-    sends = []
-    for q in range(2):
-        for c in range(2):
-            out = None
-            for j in range(BANDS):
-                t, s = divmod(BRANCHES * j, LANES)
-                tops = [8 * (g * BANDS + j) for g in range(BANDS // 8)]
-                piece = jnp.concatenate([mixed[q, top : top + 8, :] for top in tops], 0)
-                piece = turned(piece, s - SLOT * c)
-                out = piece if out is None else jnp.where(lane >= s, piece, out)
-                if s + BRANCHES >= LANES:
-                    ready[q, c, :, t * LANES : (t + 1) * LANES] = out
-                    out = piece if s + BRANCHES > LANES else None
-            sends.append(pltpu.make_async_copy(ready.at[q, c], o_ref.at[q, c], sems.at[q, c]))
-            sends[-1].start()
+        sends[-1].start()
     for send in sends:
         send.wait()
 
@@ -254,10 +247,8 @@
         rotate_kernel,
         out_shape=vmem((per_device, 2, BANDS, BANDS * BRANCHES), jnp.float32),
         scratch_shapes=[
-            pltpu.VMEM((per_device, BANDS * BANDS, LANES), jnp.float32),
-            pltpu.VMEM((per_device, BANDS * BANDS, LANES), jnp.float32),
             pltpu.VMEM((per_device, 2, BANDS, BANDS * BRANCHES), jnp.float32),
-            pltpu.SemaphoreType.DMA((per_device, 2)),
+            pltpu.SemaphoreType.DMA((BANDS // 8,)),
         ],
         out_specs=pl.BlockSpec(memory_space=pl.ANY),
         compiler_params=room(16),

time: 68.8 us -> 68.6 us (level)
  no operation moved by 1% of the time
where the time goes in v8:
time: 68.6 us; the launch traced here: 68.1 us
  blocking collectives  24.9 us (36%)
  starting transfers between devices  17.2 us (25%)
  waiting for transfers between devices  13.5 us (20%)
  Pallas kernels  5.13 us (7%)
  local copies, waits for them, and re-layouts  3.99 us (6%)
  other arithmetic  1.77 us (3%)
  between operations  0.79 us (1%)
  matrix products  0.78 us (1%)
    all_to_all x1, blocking collectives, local(): lax.all_to_all(fourier, AXES, split_axis=0, concat_axis=0, tiled=True)  24.9 us
    all_to_all x1, starting transfers between devices, local(): near = lax.all_to_all(sent, 'pb', split_axis=0, concat_axis=0, tiled=True)  12.7 us
    all_to_all x1, waiting for transfers between devices, local(): lax.all_to_all(packed, 'rp', split_axis=0, concat_axis=0, tiled=True)  7.99 us
    all_to_all x1, waiting for transfers between devices, local(): near = lax.all_to_all(sent, 'pb', split_axis=0, concat_axis=0, tiled=True)  5.55 us
    all_to_all x1, starting transfers between devices, local(): lax.all_to_all(packed, 'rp', split_axis=0, concat_axis=0, tiled=True)  4.44 us
    pallas_call x1, Pallas kernels, local(): pl.pallas_call(rotate_kernel, out_shape=vmem((per_device, 2, BANDS, BANDS...  2.18 us
    pallas_call x1, Pallas kernels, local(): pl.pallas_call(fourier_kernel, out_shape=vmem((devices, 3, per_device, LA...  1.91 us
  transfers between devices with their start and end apart: 2, of which 2 were waited for; matrix products, arithmetic and copies ran while one was open for 7% of the time, Pallas kernels for 2%

profile of v8, /device:TPU:1, one launch (start us, length us, event | category | flops | bytes accessed | tf_op | source)
XLA Modules:
  0.0 68.1 jit_solution(10474142781845252290)
XLA Ops:
  0.0 0.0 copy-start
  0.0 0.0 copy-start.1
  0.0 1.4 %broadcast_in_dim.20 = s32[32,3,2]{1,2,0:T(2,128)} broadcast(s32[3,2]{0,1:T(2,128)} %param.11), dimensions={1,2} | broadcast | bytes 792 | tf_op jit(solution)/shard_map/broadcast_in_dim | solution.py:182
  1.4 12.7 %all-to-all-start = ((s32[32,3,2]{1,2,0:T(2,128)}), s32[32,3,2]{1,2,0:T(2,128)S(1)}, u32[]{:S(2)}, u32[]{:S(2)}) async-start(s32[32,3,2]{1,2,0:T(2,128)} %broadcast_in_dim.20), calls=%async_computation | async-start | bytes 65536 | tf_op jit(solution)/shard_map/all_to_all | solution.py:183
  14.1 0.8 %copy.21 = bf16[2,2,36,36]{3,2,0,1:T(8,128)(2,1)S(1)} copy(bf16[2,2,36,36]{3,1,2,0:T(2,128)(2,1)} %param.15) | data formatting | bytes 20736 | tf_op args[6]
  15.0 0.7 %slice_bitcast_fusion = (bf16[2,32,1,32]{3,1,0,2:T(8,128)(2,1)S(1)}, bf16[2,32,1,32]{3,1,0,2:T(8,128)(2,1)S(1)}) fusion(bf16[2,2,32,32]{3,2,1,0:T(8,128)(2,1)} %param.14), kind=kLoop, calls=%fused_computation.23 | loop fusion | bytes 16384 | tf_op jit(solution)/shard_map/squeeze | solution.py:204
  15.7 0.7 %fusion.22 = bf16[2,32,1,32]{3,1,0,2:T(8,128)(2,1)S(1)} fusion(bf16[2,2,32,32]{3,2,1,0:T(8,128)(2,1)} %param.14), kind=kLoop, calls=%fused_computation.41 | loop fusion | flops 2048 | bytes 8192 | tf_op jit(solution)/shard_map/neg | solution.py:205
  16.5 0.7 %multiply_convert_fusion = bf16[3,1024]{1,0:T(4,128)(2,1)S(1)} fusion(s32[3,1024]{1,0:T(4,128)} %param.10), kind=kLoop, calls=%fused_computation.27 | loop fusion | flops 9216 | bytes 18432 | tf_op jit(solution)/shard_map/convert
  17.2 0.0 copy-done.1
  17.2 1.0 %pack.1 = bf16[8,296,128]{2,1,0:T(8,128)(2,1)} custom-call(bf16[256,1152]{1,0:T(8,128)(2,1)S(1)} %bitcast.61), custom_call_target="tpu_custom_call" | custom-call | tf_op jit(solution)/shard_map/pack/pallas_call | solution.py:186
  18.3 5.6 %all-to-all-done = s32[32,3,2]{1,2,0:T(2,128)S(1)} async-done(((s32[32,3,2]{1,2,0:T(2,128)}), s32[32,3,2]{1,2,0:T(2,128)S(1)}, u32[]{:S(2)}, u32[]{:S(2)}) %all-to-all-start) | async-done | bytes 800 | tf_op jit(solution)/shard_map/all_to_all | solution.py:183
  23.9 0.1 copy.26
  23.9 0.6 broadcast_dynamic-update-slice_fusion
  24.6 4.4 %all-to-all-start.1 = ((bf16[8,296,128]{2,1,0:T(8,128)(2,1)}), bf16[8,296,128]{2,1,0:T(8,128)(2,1)S(1)}, u32[]{:S(2)}, u32[]{:S(2)}) async-start(bf16[8,296,128]{2,1,0:T(8,128)(2,1)} %broadcast_dynamic-update-slice_fusion), calls=%async_computation.1 | async-start | bytes 1212416 | tf_op jit(solution)/shard_map/all_to_all | solution.py:226
  29.0 0.1 copy.19
  29.1 0.1 dot_general.20
  29.2 0.1 reshape_reshape.3
  29.3 0.1 copy.20
  30.1 0.1 maximum_maximum_fusion.e_ref
  30.2 0.1 broadcast_compare_fusion
  30.3 0.2 fusion.2
  30.5 0.0 copy-done
  30.5 0.2 fusion.4
  30.7 0.4 fusion.u_ref
  31.1 8.0 %all-to-all-done.1.x_ref = bf16[8,296,128]{2,1,0:T(8,128)(2,1)S(1)} async-done(((bf16[8,296,128]{2,1,0:T(8,128)(2,1)}), bf16[8,296,128]{2,1,0:T(8,128)(2,1)S(1)}, u32[]{:S(2)}, u32[]{:S(2)}) %all-to-all-start.1) | async-done | bytes 606240 | tf_op jit(solution)/shard_map/all_to_all | solution.py:226
  39.1 1.9 %fourier.1 = bf16[256,3,2,128]{3,2,1,0:T(2,128)(2,1)S(1)} custom-call(bf16[8,296,128]{2,1,0:T(8,128)(2,1)S(1)} %all-to-all-done.1.x_ref, bf16[8,1024]{1,0:T(8,128)(2,1)S(1)} %pad.16.r_ref), custom_call_target="tpu_custom_call" | custom-call | tf_op jit(solution)/shard_map/fourier/pallas_call | solution.py:230
  41.0 24.9 %all_to_all.15 = bf16[256,3,2,128]{3,2,1,0:T(2,128)(2,1)S(1)} all-to-all(bf16[256,3,2,128]{3,2,1,0:T(2,128)(2,1)S(1)} %fourier.1), channel_id=1, replica_groups=mesh['rp'=8,'pb'=32] {'rp','pb'}, dimensions={0} | all-to-all | bytes 786432 | tf_op jit(solution)/shard_map/all_to_all | solution.py:243
  65.9 2.2 %rotate.1 = f32[2,2,32,1152]{3,2,1,0:T(8,128)} custom-call(bf16[8,32,3,2,128]{4,3,2,1,0:T(2,128)(2,1)S(1)} %bitcast.60, bf16[128,128]{1,0:T(8,128)(2,1)S(1)} %bitcast.62, bf16[2,128,256]{2,1,0:T(8,128)(2,1)S(1)} %maximum_maximum_fusion.e_ref, bf16[2,256,256]{2,1,0:T(8,128)(2,1)S(1)} %fusion.u_ref), custom_call_target="tpu_custom_call" | custom-call | tf_op jit(solution)/shard_map/rotate/pallas_call | solution.py:246
  (13 shorter events, 0.2 us)
Async XLA Ops:
  0.0 30.5 %copy-start = (bf16[8,2,32,32]{3,2,1,0:T(8,128)(2,1)S(1)}, bf16[8,2,32,32]{3,2,1,0:T(8,128)(2,1)}, u32[]{:S(2)}) copy-start(bf16[8,2,32,32]{3,2,1,0:T(8,128)(2,1)} %param.13) | copy-start | bytes 98308
  0.0 17.2 %copy-start.1 = (bf16[2,128,1,1152]{3,1,2,0:T(8,128)(2,1)S(1)}, bf16[2,128,1,1152]{3,1,2,0:T(8,128)(2,1)}, u32[]{:S(2)}) copy-start(bf16[2,128,1,1152]{3,1,2,0:T(8,128)(2,1)} %param.9) | copy-start | bytes 1769476
  1.4 22.5 %all-to-all-start = ((s32[32,3,2]{1,2,0:T(2,128)}), s32[32,3,2]{1,2,0:T(2,128)S(1)}, u32[]{:S(2)}, u32[]{:S(2)}) async-start(s32[32,3,2]{1,2,0:T(2,128)} %broadcast_in_dim.20), calls=%async_computation | async-start | bytes 65536 | tf_op jit(solution)/shard_map/all_to_all | solution.py:183
  24.6 14.5 %all-to-all-start.1 = ((bf16[8,296,128]{2,1,0:T(8,128)(2,1)}), bf16[8,296,128]{2,1,0:T(8,128)(2,1)S(1)}, u32[]{:S(2)}, u32[]{:S(2)}) async-start(bf16[8,296,128]{2,1,0:T(8,128)(2,1)} %broadcast_dynamic-update-slice_fusion), calls=%async_computation.1 | async-start | bytes 1212416 | tf_op jit(solution)/shard_map/all_to_all | solution.py:226
